TPU v7x, 32 devices: a whole 2x2x4 slice. The times are simulated.
32 devices in a mesh: dp: 8 (over z, core), tensor: 4 (over y, x).
Axes of the slice: x: 2, y: 2, z: 4, core: 2. Of those that a mesh axis runs over, the one named last changes fastest.
Arguments:
- tokens: bfloat16 [1024, 2048], P(('dp', 'tensor')), may hold values from -6 to 6
- gate_weight: bfloat16 [2048, 8192], P(None, 'tensor'), may hold values from -0.125 to 0.125
- up_act: bfloat16 [1024, 8192], P('dp', 'tensor'), may hold values from -6 to 6
- cotangent: bfloat16 [1024, 8192], P('dp', 'tensor'), may hold values from -6 to 6
- moment1: bfloat16 [2048, 8192], P('dp', 'tensor'), may hold values from -0.359375 to 0.359375
- moment2: bfloat16 [2048, 8192], P('dp', 'tensor'), may hold values from 0.0039978027 to 0.039794922
Outputs:
- in_grad: bfloat16 [1024, 2048], P(('dp', 'tensor'))
- up_grad: bfloat16 [1024, 8192], P('dp', 'tensor')
- new_moment1: bfloat16 [2048, 8192], P('dp', 'tensor')
- new_moment2: bfloat16 [2048, 8192], P('dp', 'tensor')
- update: float32 [2048, 8192], P('dp', 'tensor')
All inputs are finite; a program needn't handle non-finite values.
Results may differ from a plain program's by a relative error of at most 0.015.
Values may be sent and summed in bfloat16 or wider, within the bound.
A program may use at most 64 MiB of HBM per device.

v0:
```python
import functools
import math

import jax
import jax.numpy as jnp
from jax import lax
from jax.experimental import pallas as pl
from jax.experimental.pallas import tpu as pltpu
from jax.sharding import PartitionSpec as P

MESH = pl.DeviceIdType.MESH
F32, BF16 = jnp.float32, jnp.bfloat16
CORES = 2
WIDE = 512
VMEM_BUDGET = 48 * 2**20


def adam(grad, moment1, moment2):
    first = 0.9 * moment1.astype(F32) + 0.1 * grad
    second = 0.95 * moment2.astype(F32) + 0.05 * grad * grad
    return first, second, first / (jnp.sqrt(second) + 1e-08)


def activation_grads(gate_pre, cot, up):
    sig = jax.nn.sigmoid(gate_pre)
    cot = cot.astype(F32)
    up_grad = (cot * gate_pre * sig).astype(BF16)
    gate_grad = (cot * up.astype(F32) * sig * (1.0 + gate_pre * (1.0 - sig))).astype(BF16)
    return up_grad, gate_grad


def kernel(ndp, nt, tok, w, up, cot, m1, m2, in_grad, up_grad, nm1, nm2, upd,
           tg, xg, xt, wv, upv, cotv, m1v, m2v, gall, term, termr,
           loc_sem, w_sem, tg_s, tg_r, x1_s, x1_r, x2_s, x2_r,
           us, ur, ds, dr, ps, pr, qs, qr, ts, tr):
    d, t = lax.axis_index("dp"), lax.axis_index("tensor")
    z, core = d // CORES, d % CORES
    nz = ndp // CORES
    mate = d + 1 - 2 * core
    m, dw = tok.shape
    g, hid = up.shape
    rw = m1.shape[0]
    nc, _, hc = wv.shape
    scale = 1.0 / math.sqrt(ndp * g)

    def rdma(src, dst, s, r, dp, tn):
        return pltpu.make_async_remote_copy(
            src_ref=src, dst_ref=dst, send_sem=s, recv_sem=r, device_id=(dp, tn), device_id_type=MESH)

    mine = pl.ds(pl.multiple_of(t * m, m), m)
    loads = [
        pltpu.make_async_copy(tok, tg.at[mine], loc_sem.at[0]),
        pltpu.make_async_copy(tok.at[:, pl.ds(pl.multiple_of(d * rw, rw), rw)], xg.at[d, t], loc_sem.at[1]),
        pltpu.make_async_copy(cot, cotv, loc_sem.at[2]),
        pltpu.make_async_copy(up, upv, loc_sem.at[3]),
        pltpu.make_async_copy(m1, m1v, loc_sem.at[4]),
        pltpu.make_async_copy(m2, m2v, loc_sem.at[5]),
    ]

    def w_load(c):
        return pltpu.make_async_copy(w.at[:, pl.ds(pl.multiple_of(c * hc, hc), hc)], wv.at[c], w_sem.at[c])

    loads[0].start()
    loads[1].start()
    w_load(0).start()
    loads[2].start()
    loads[3].start()
    for c in range(1, nc):
        w_load(c).start()
    loads[4].start()
    loads[5].start()

    barrier = pltpu.get_barrier_semaphore()
    for k in range(1, nt):
        pl.semaphore_signal(barrier, inc=1, device_id=(d, lax.rem(t + k, nt)), device_id_type=MESH)
    for k in range(1, ndp):
        pl.semaphore_signal(barrier, inc=1, device_id=(lax.rem(d + k, ndp), t), device_id_type=MESH)
    loads[0].wait()
    loads[1].wait()
    pl.semaphore_wait(barrier, nt - 1 + ndp - 1)

    def tok_copy(k):
        return rdma(tg.at[mine], tg.at[mine], tg_s.at[k], tg_r.at[k], d, lax.rem(t + k, nt))

    def tok_recv(k):
        rows = pl.ds(pl.multiple_of(lax.rem(t + nt - k, nt) * m, m), m)
        return rdma(tg.at[rows], tg.at[rows], tg_s.at[k], tg_r.at[k], d, lax.rem(t + k, nt))

    def x1_copy(k):
        to = lax.rem(d + k, ndp)
        return rdma(tg.at[mine, pl.ds(pl.multiple_of(to * rw, rw), rw)], xg.at[d, t], x1_s.at[k], x1_r.at[k], to, t)

    def x1_recv(k):
        origin = lax.rem(d + ndp - k, ndp)
        return rdma(xg.at[origin, t], xg.at[origin, t], x1_s.at[k], x1_r.at[k], lax.rem(d + k, ndp), t)

    def x2_copy(k):
        return rdma(xg.at[:, t], xg.at[:, t], x2_s.at[k], x2_r.at[k], d, lax.rem(t + k, nt))

    def x2_recv(k):
        origin = lax.rem(t + nt - k, nt)
        return rdma(xg.at[:, origin], xg.at[:, origin], x2_s.at[k], x2_r.at[k], d, lax.rem(t + k, nt))

    for k in range(1, nt):
        tok_copy(k).start()
    for k in range(1, ndp):
        x1_copy(k).start()
    loads[2].wait()
    loads[3].wait()
    for k in range(1, nt):
        tok_recv(k).wait_recv()

    def block(c, chip, cr):
        return gall.at[c, pl.ds(pl.multiple_of((chip * CORES + cr) * g, g), g)]

    def up_copy(s, c):
        b = block(c, z - s, core)
        return rdma(b, b, us.at[s, c], ur.at[s, c], d + CORES, t)

    def down_copy(s, c):
        b = block(c, z + s, core)
        return rdma(b, b, ds.at[s, c], dr.at[s, c], d - CORES, t)

    def up_recv(s, c):
        b = block(c, z - s, core)
        return rdma(b, b, us.at[s - 1, c], ur.at[s - 1, c], d + CORES, t)

    def down_recv(s, c):
        b = block(c, z + s, core)
        return rdma(b, b, ds.at[s - 1, c], dr.at[s - 1, c], d - CORES, t)

    def mate_copy(s, c, low):
        b = block(c, z - s if low else z + s, core)
        return rdma(b, b, (ps if low else qs).at[s, c], (pr if low else qr).at[s, c], mate, t)

    def mate_recv(s, c, low):
        b = block(c, z - s if low else z + s, 1 - core)
        return rdma(b, b, (ps if low else qs).at[s, c], (pr if low else qr).at[s, c], mate, t)

    def hop(s, c):
        @pl.when(z - s >= 0)
        def _():
            if s > 0:
                up_recv(s, c).wait_recv()
            if s < nz - 1:
                @pl.when(z + 1 < nz)
                def _():
                    up_copy(s, c).start()
            mate_copy(s, c, True).start()

        @pl.when(z + s < nz)
        def _():
            if s > 0:
                down_recv(s, c).wait_recv()
            if s < nz - 1:
                @pl.when(z >= 1)
                def _():
                    down_copy(s, c).start()
            if s > 0:
                mate_copy(s, c, False).start()

    @pl.loop(0, nc)
    def _(c):
        w_load(c).wait()
        cols = pl.ds(pl.multiple_of(c * hc, hc), hc)
        gate_pre = jnp.dot(tg[...], wv[c], preferred_element_type=F32)
        ug, gg = activation_grads(gate_pre, cotv[:, cols], upv[:, cols])
        gall[c, pl.ds(pl.multiple_of(d * g, g), g), :] = gg
        up_grad[:, cols] = ug
        hop(0, c)

    for k in range(1, ndp):
        x1_recv(k).wait_recv()
    for k in range(1, nt):
        x2_copy(k).start()

    part = dw // nc

    @pl.loop(0, nc)
    def _(n):
        if nz > 1:
            hop(1, n)
        rows = pl.ds(pl.multiple_of(n * part, part), part)
        own = pl.ds(pl.multiple_of(d * g, g), g)
        total = jnp.zeros((g, part), F32)
        for c in range(nc):
            total += lax.dot_general(
                gall[c, own, :], wv[c, rows, :], (((1,), (1,)), ((), ())), preferred_element_type=F32)
        term[:, rows] = total.astype(BF16)

    for k in range(1, nt):
        x2_recv(k).wait_recv()
    for i in range(ndp):
        xt[:, i * g:(i + 1) * g] = xg[i].reshape(g, rw).T

    def term_copy(k):
        to = lax.rem(t + k, nt)
        return rdma(term.at[pl.ds(pl.multiple_of(to * m, m), m)], termr.at[k], ts.at[k], tr.at[k], d, to)

    for k in range(1, nt):
        term_copy(k).start()
    for s in range(2, nz - 1):
        @pl.loop(0, nc)
        def _(c):
            hop(s, c)
    total = term[mine, :].astype(F32)
    for k in range(1, nt):
        term_copy(k).wait_recv()
        total += termr[k].astype(F32)
    in_grad[...] = total.astype(BF16)
    loads[4].wait()
    loads[5].wait()

    @pl.loop(0, nc)
    def _(c):
        if nz > 2:
            hop(nz - 1, c)
        for s in range(nz):
            @pl.when(z - s >= 0)
            def _():
                mate_recv(s, c, True).wait_recv()
            if s > 0:
                @pl.when(z + s < nz)
                def _():
                    mate_recv(s, c, False).wait_recv()
        cols = pl.ds(pl.multiple_of(c * hc, hc), hc)
        grad = jnp.dot(xt[...], gall[c], preferred_element_type=F32) * scale
        first, second, step = adam(grad, m1v[:, cols], m2v[:, cols])
        nm1[:, cols] = first.astype(BF16)
        nm2[:, cols] = second.astype(BF16)
        upd[:, cols] = step

    for k in range(1, nt):
        tok_copy(k).wait_send()
        x2_copy(k).wait_send()
        term_copy(k).wait_send()
    for k in range(1, ndp):
        x1_copy(k).wait_send()

    @pl.loop(0, nc)
    def _(c):
        for s in range(nz):
            @pl.when(z - s >= 0)
            def _():
                mate_copy(s, c, True).wait_send()
                if s < nz - 1:
                    @pl.when(z + 1 < nz)
                    def _():
                        up_copy(s, c).wait_send()

            @pl.when(z + s < nz)
            def _():
                if s > 0:
                    mate_copy(s, c, False).wait_send()
                if s < nz - 1:
                    @pl.when(z >= 1)
                    def _():
                        down_copy(s, c).wait_send()


def fused(ndp, nt, tokens, gate_weight, up_act, cotangent, moment1, moment2):
    m, dw = tokens.shape
    g, hid = up_act.shape
    rw = moment1.shape[0]
    nc, nz = hid // WIDE, ndp // CORES
    any_spec, vmem = pl.BlockSpec(memory_space=pltpu.HBM), pl.BlockSpec(memory_space=pltpu.VMEM)
    dma = pltpu.SemaphoreType.DMA
    results = (((m, dw), BF16), ((g, hid), BF16), ((rw, hid), BF16), ((rw, hid), BF16), ((rw, hid), F32))
    held = pl.pallas_call(
        functools.partial(kernel, ndp, nt),
        out_shape=tuple(pltpu.VMEM(shape, dtype) for shape, dtype in results),
        in_specs=[any_spec] * 6,
        out_specs=(vmem,) * 5,
        scratch_shapes=[
            pltpu.VMEM((g, dw), BF16),
            pltpu.VMEM((ndp, nt, m, rw), BF16),
            pltpu.VMEM((rw, ndp * g), BF16),
            pltpu.VMEM((nc, dw, WIDE), BF16),
            pltpu.VMEM((g, hid), BF16),
            pltpu.VMEM((g, hid), BF16),
            pltpu.VMEM((rw, hid), BF16),
            pltpu.VMEM((rw, hid), BF16),
            pltpu.VMEM((nc, ndp * g, WIDE), BF16),
            pltpu.VMEM((g, dw), BF16),
            pltpu.VMEM((nt, m, dw), BF16),
            dma((6,)), dma((nc,)),
            dma((nt,)), dma((nt,)),
            dma((ndp,)), dma((ndp,)),
            dma((nt,)), dma((nt,)),
            dma((nz, nc)), dma((nz, nc)), dma((nz, nc)), dma((nz, nc)),
            dma((nz, nc)), dma((nz, nc)), dma((nz, nc)), dma((nz, nc)),
            dma((nt,)), dma((nt,)),
        ],
        compiler_params=pltpu.CompilerParams(
            collective_id=0, has_side_effects=True, vmem_limit_bytes=VMEM_BUDGET),
    )(*(pltpu.with_memory_space_constraint(x, pltpu.HBM)
        for x in (tokens, gate_weight, up_act, cotangent, moment1, moment2)))
    return pl.pallas_call(
        write_out,
        out_shape=tuple(pltpu.HBM(shape, dtype) for shape, dtype in results),
        in_specs=[vmem] * 5,
        out_specs=(any_spec,) * 5,
        scratch_shapes=[dma((5,))],
        compiler_params=pltpu.CompilerParams(vmem_limit_bytes=2**20),
    )(*(pltpu.with_memory_space_constraint(x, pltpu.VMEM) for x in held))


def write_out(*refs):
    sems = refs[-1]
    copies = [pltpu.make_async_copy(refs[i], refs[5 + i], sems.at[i]) for i in range(5)]
    for copy in reversed(copies):
        copy.start()
    for copy in copies:
        copy.wait()


def plain(ndp, nt, tokens, gate_weight, up_act, cotangent, moment1, moment2):
    gathered = lax.all_gather(tokens, "tensor", axis=0, tiled=True)
    gate_pre = jnp.dot(gathered, gate_weight, preferred_element_type=F32)
    up_grad, gate_grad = activation_grads(gate_pre, cotangent, up_act)
    term = lax.dot_general(
        gate_grad, gate_weight, (((1,), (1,)), ((), ())), preferred_element_type=F32).astype(BF16)
    in_grad = lax.psum_scatter(term, "tensor", scatter_dimension=0, tiled=True)
    partial_value = lax.dot_general(
        gathered, gate_grad, (((0,), (0,)), ((), ())), preferred_element_type=F32).astype(BF16)
    shard = lax.psum_scatter(partial_value.astype(F32), "dp", scatter_dimension=0, tiled=True)
    first, second, update = adam(shard * (1.0 / math.sqrt(ndp * gathered.shape[0])), moment1, moment2)
    return in_grad, up_grad, first.astype(BF16), second.astype(BF16), update


def local(ndp, nt, *args):
    (m, dw), (g, hid), rw = args[0].shape, args[2].shape, args[4].shape[0]
    need = (2 * dw * hid + 2 * ndp * g * (hid + 2 * rw) + 12 * g * hid + 16 * rw * hid + 16 * g * dw)
    fits = (need <= VMEM_BUDGET and ndp % CORES == 0 and ndp > CORES and nt > 1 and hid % WIDE == 0
            and g % 128 == 0 and rw % 128 == 0 and m % 16 == 0 and dw % (128 * (hid // WIDE)) == 0)
    return (fused if fits else plain)(ndp, nt, *args)


def solution(mesh):
    both = P("dp", "tensor")
    rows = P(("dp", "tensor"), None)
    return jax.shard_map(
        functools.partial(local, mesh.shape["dp"], mesh.shape["tensor"]),
        mesh=mesh,
        in_specs=(rows, P(None, "tensor"), both, both, both, both),
        out_specs=(rows, both, both, both, both),
        check_vma=False,
    )
```

profile of v0, /device:TPU:0, one launch (start us, length us, event | category | flops | bytes accessed | tf_op | source)
XLA Modules:
  0.0 55.1 jit_solution(16665282431480594121)
XLA Ops:
  0.6 52.2 %shard_map.101 = (bf16[32,2048]{1,0:T(8,128)(2,1)S(1)}, bf16[128,2048]{1,0:T(8,128)(2,1)S(1)}, bf16[256,2048]{1,0:T(8,128)(2,1)S(1)}, bf16[256,2048]{1,0:T(8,128)(2,1)S(1)}, f32[256,2048]{1,0:T(8,128)S(1)}) custom-call(bf16[32,2048]{1,0:T(8,128)(2,1)} %tok.1, bf16[2048,2048]{1,0:T(8,128)(2,1)} %w.1, bf16[128,2048]{1,0:T(8,128)(2,1)} %up.1, ...), custom_call_target="tpu_custom_call" | custom-call | tf_op jit(solution)/shard_map/pallas_call | solution.py:269
  52.8 2.2 %shard_map.102 = (bf16[32,2048]{1,0:T(8,128)(2,1)}, bf16[128,2048]{1,0:T(8,128)(2,1)}, bf16[256,2048]{1,0:T(8,128)(2,1)}, bf16[256,2048]{1,0:T(8,128)(2,1)}, f32[256,2048]{1,0:T(8,128)}) custom-call(bf16[32,2048]{1,0:T(8,128)(2,1)S(1)} %get-tuple-element.10.refs_0_, bf16[128,2048]{1,0:T(8,128)(2,1)S(1)} %get-tuple-element.11.refs_1_, ...), custom_call_target="tpu_custom_call" | custom-call | tf_op jit(solution)/shard_map/pallas_call | solution.py:298
where the time goes:
time: 55.2 us; the launch traced here: 55.1 us
  Pallas kernels  54.4 us (99%)
  between operations  0.64 us (1%)
    pallas_call x1, Pallas kernels, fused(): pl.pallas_call(functools.partial(kernel, ndp, nt), out_shape=tuple((pltpu...  52.2 us
    pallas_call x1, Pallas kernels, fused(): pl.pallas_call(write_out, out_shape=tuple((pltpu.HBM(shape, dtype) for sh...  2.24 us

commit v1 on v0

v1 whole, which is shorter than its diff:
```python
import functools
import math

import jax
import jax.numpy as jnp
from jax import lax
from jax.experimental import pallas as pl
from jax.experimental.pallas import tpu as pltpu
from jax.sharding import PartitionSpec as P

MESH = pl.DeviceIdType.MESH
F32, BF16 = jnp.float32, jnp.bfloat16
CORES = 2
CHIPS = 4
WIDE = 256
VMEM_BUDGET = 48 * 2**20


def adam(grad, moment1, moment2):
    first = 0.9 * moment1.astype(F32) + 0.1 * grad
    second = 0.95 * moment2.astype(F32) + 0.05 * grad * grad
    return first, second, first / (jnp.sqrt(second) + 1e-08)


def activation_grads(gate_pre, cot, up):
    sig = jax.nn.sigmoid(gate_pre)
    cot = cot.astype(F32)
    up_grad = (cot * gate_pre * sig).astype(BF16)
    gate_grad = (cot * up.astype(F32) * sig * (1.0 + gate_pre * (1.0 - sig))).astype(BF16)
    return up_grad, gate_grad


def flip(t, k):
    bit = 1
    while bit <= k:
        if k & bit:
            t = t + bit - 2 * bit * lax.rem(t // bit, 2)
        bit *= 2
    return t


def kernel(ndp, nt, tok, w, up, cot, m1, m2, in_grad, up_grad, nm1, nm2, upd,
           tg, xg, xt, wv, upv, cotv, m1v, m2v, gall, term, termr,
           loc_sem, w_sem, cu_sem, tg_s, tg_r, x1_s, x1_r, x2_s, x2_r,
           zs, zr, fs, ms, mr, ts, tr):
    d, t = lax.axis_index("dp"), lax.axis_index("tensor")
    z, core = d // CORES, lax.rem(d, CORES)
    mate = d + 1 - 2 * core
    m, dw = tok.shape
    g, hid = up.shape
    rw = m1.shape[0]
    nc, _, hc = wv.shape
    scale = 1.0 / math.sqrt(ndp * g)

    half = z // 2
    near = z + 1 - 2 * lax.rem(z, 2)
    across = 2 - half
    far = 3 - 3 * half
    outer = lax.rem(z + half + 1, 2)
    chips = (near, across, far, z)
    NEAR, ACROSS, FAR, OWN = range(4)

    def rdma(src, dst, s, r, dp, tn):
        return pltpu.make_async_remote_copy(
            src_ref=src, dst_ref=dst, send_sem=s, recv_sem=r, device_id=(dp, tn), device_id_type=MESH)

    def rows_of(i, size):
        return pl.ds(pl.multiple_of(i * size, size), size)

    load_tok = pltpu.make_async_copy(tok, tg.at[0:m], loc_sem.at[0])
    load_x = pltpu.make_async_copy(tok.at[:, rows_of(d, rw)], xg.at[0, d], loc_sem.at[1])
    load_m1 = pltpu.make_async_copy(m1, m1v, loc_sem.at[2])
    load_m2 = pltpu.make_async_copy(m2, m2v, loc_sem.at[3])

    def w_load(c):
        return pltpu.make_async_copy(w.at[:, rows_of(c, hc)], wv.at[c], w_sem.at[c])

    def cu_loads(k):
        src = rows_of(flip(t, k), m)
        dst = pl.ds(k * m, m)
        return (pltpu.make_async_copy(cot.at[src], cotv.at[dst], cu_sem.at[0, k]),
                pltpu.make_async_copy(up.at[src], upv.at[dst], cu_sem.at[1, k]))

    load_tok.start()
    w_load(0).start()
    for copy in cu_loads(0):
        copy.start()
    for c in range(1, nc):
        w_load(c).start()
    load_x.start()

    barrier = pltpu.get_barrier_semaphore()
    for k in range(1, ndp):
        pl.semaphore_signal(barrier, inc=1, device_id=(lax.rem(d + k, ndp), t), device_id_type=MESH)
    for k in range(1, nt):
        pl.semaphore_signal(barrier, inc=1, device_id=(d, flip(t, k)), device_id_type=MESH)
    for k in range(1, nt):
        for copy in cu_loads(k):
            copy.start()
    load_m1.start()
    load_m2.start()

    def tok_copy(k):
        return rdma(tg.at[0:m], tg.at[k * m:(k + 1) * m], tg_s.at[k], tg_r.at[k], d, flip(t, k))

    def x1_copy(k):
        to = lax.rem(d + k, ndp)
        return rdma(tg.at[0:m, rows_of(to, rw)], xg.at[0, d], x1_s.at[k], x1_r.at[k], to, t)

    def x1_recv(k):
        origin = lax.rem(d + ndp - k, ndp)
        return rdma(xg.at[0, origin], xg.at[0, origin], x1_s.at[k], x1_r.at[k], lax.rem(d + k, ndp), t)

    def x2_copy(k):
        return rdma(xg.at[0], xg.at[k], x2_s.at[k], x2_r.at[k], d, flip(t, k))

    def term_copy(k):
        return rdma(term.at[k * m:(k + 1) * m], termr.at[k], ts.at[k], tr.at[k], d, flip(t, k))

    def block(c, part, chip, cr):
        start = pl.multiple_of((chip * CORES + cr) * g, g) + (m if part else 0)
        return gall.at[c, pl.ds(pl.multiple_of(start, m), g - m if part else m)]

    def own_copy(c, part, to):
        b = block(c, part, z, core)
        if to == NEAR:
            return rdma(b, b, zs.at[0, part, c], zr.at[NEAR, part, c], near * CORES + core, t)
        return rdma(b, b, zs.at[1, part, c], zr.at[ACROSS + outer, part, c], across * CORES + core, t)

    def arrival(c, part, origin):
        b = block(c, part, chips[origin], core)
        return rdma(b, b, zs.at[0, part, c], zr.at[origin, part, c], near * CORES + core, t)

    def forward_copy(c, part, origin):
        b = block(c, part, chips[origin], core)
        return rdma(b, b, fs.at[origin - 1, part, c], zr.at[origin, part, c], near * CORES + core, t)

    def mate_copy(c, part, origin):
        b = block(c, part, chips[origin], core)
        return rdma(b, b, ms.at[origin, part, c], mr.at[origin, part, c], mate, t)

    def mate_recv(c, part, origin):
        b = block(c, part, chips[origin], 1 - core)
        return rdma(b, b, ms.at[origin, part, c], mr.at[origin, part, c], mate, t)

    def take(c, part, origin):
        arrival(c, part, origin).wait_recv()
        if origin != NEAR:
            @pl.when(outer == 0)
            def _():
                forward_copy(c, part, origin).start()
        mate_copy(c, part, origin).start()

    def grads(c, part):
        here = slice(m, g) if part else slice(0, m)
        cols = rows_of(c, hc)
        gate_pre = jnp.dot(tg[here], wv[c], preferred_element_type=F32)
        ug, gg = activation_grads(gate_pre, cotv[here, cols], upv[here, cols])
        start = pl.multiple_of(d * g, g) + (m if part else 0)
        gall[c, pl.ds(pl.multiple_of(start, m), g - m if part else m), :] = gg
        for k in range(1, nt) if part else (0,):
            low = (k - 1) * m if part else 0
            up_grad[rows_of(flip(t, k), m), cols] = ug[low:low + m]

    def send_own(c, part):
        own_copy(c, part, ACROSS).start()
        own_copy(c, part, NEAR).start()
        mate_copy(c, part, OWN).start()

    load_tok.wait()
    for copy in cu_loads(0):
        copy.wait()

    @pl.loop(0, nc)
    def _(c):
        w_load(c).wait()
        grads(c, 0)

    load_x.wait()
    pl.semaphore_wait(barrier, ndp - 1 + nt - 1)
    for k in range(1, nt):
        tok_copy(k).start()

    @pl.loop(0, nc)
    def _(c):
        send_own(c, 0)

    for k in range(1, ndp):
        x1_copy(k).start()
    for k in range(1, nt):
        for copy in cu_loads(k):
            copy.wait()

    @pl.when(outer == 0)
    def _():
        @pl.loop(0, nc)
        def _(c):
            take(c, 0, ACROSS)
            take(c, 0, FAR)

    for k in range(1, nt):
        tok_copy(k).wait_recv()

    @pl.loop(0, nc)
    def _(c):
        grads(c, 1)

        @pl.when(c > 0)
        def _():
            send_own(c - 1, 1)

    part = dw // nc

    def term_part(n):
        rows = rows_of(n, part)
        own = rows_of(d, g)
        total = jnp.zeros((g, part), F32)
        for c in range(nc):
            total += lax.dot_general(
                gall[c, own, :], wv[c, rows, :], (((1,), (1,)), ((), ())), preferred_element_type=F32)
        term[:, rows] = total.astype(BF16)

    term_part(0)
    send_own(nc - 1, 1)
    for k in range(1, ndp):
        x1_recv(k).wait_recv()
    for k in range(1, nt):
        x2_copy(k).start()

    @pl.loop(1, nc)
    def _(n):
        term_part(n)

    @pl.when(outer == 1)
    def _():
        @pl.loop(0, nc)
        def _(c):
            take(c, 0, ACROSS)
            take(c, 0, FAR)

    for k in range(1, nt):
        term_copy(k).start()

    @pl.loop(0, nc)
    def _(c):
        take(c, 0, NEAR)

    for k in range(1, nt):
        x2_copy(k).wait_recv()
    for i in range(ndp):
        xt[:, i * g:(i + 1) * g] = xg[:, i].reshape(g, rw).T

    total = term[0:m, :].astype(F32)
    for k in range(1, nt):
        term_copy(k).wait_recv()
        total += termr[k].astype(F32)
    in_grad[...] = total.astype(BF16)
    load_m1.wait()
    load_m2.wait()

    def update(c):
        for origin in range(4):
            for part in range(2):
                mate_recv(c, part, origin).wait_recv()
        cols = rows_of(c, hc)
        grad = jnp.dot(xt[...], gall[c], preferred_element_type=F32) * scale
        first, second, step = adam(grad, m1v[:, cols], m2v[:, cols])
        nm1[:, cols] = first.astype(BF16)
        nm2[:, cols] = second.astype(BF16)
        upd[:, cols] = step

    @pl.loop(0, nc + 1)
    def _(c):
        @pl.when(c < nc)
        def _():
            take(c, 1, NEAR)
            take(c, 1, ACROSS)
            take(c, 1, FAR)

        @pl.when(c > 0)
        def _():
            update(c - 1)

    for k in range(1, nt):
        tok_copy(k).wait_send()
        x2_copy(k).wait_send()
        term_copy(k).wait_send()
    for k in range(1, ndp):
        x1_copy(k).wait_send()

    @pl.loop(0, nc)
    def _(c):
        for p in range(2):
            own_copy(c, p, NEAR).wait_send()
            own_copy(c, p, ACROSS).wait_send()
            for origin in range(4):
                mate_copy(c, p, origin).wait_send()

            @pl.when(outer == 0)
            def _():
                forward_copy(c, p, ACROSS).wait_send()
                forward_copy(c, p, FAR).wait_send()


def fused(ndp, nt, tokens, gate_weight, up_act, cotangent, moment1, moment2):
    m, dw = tokens.shape
    g, hid = up_act.shape
    rw = moment1.shape[0]
    nc = hid // WIDE
    any_spec, vmem = pl.BlockSpec(memory_space=pltpu.HBM), pl.BlockSpec(memory_space=pltpu.VMEM)
    dma = pltpu.SemaphoreType.DMA
    results = (((m, dw), BF16), ((g, hid), BF16), ((rw, hid), BF16), ((rw, hid), BF16), ((rw, hid), F32))
    held = pl.pallas_call(
        functools.partial(kernel, ndp, nt),
        out_shape=tuple(pltpu.VMEM(shape, dtype) for shape, dtype in results),
        in_specs=[any_spec] * 6,
        out_specs=(vmem,) * 5,
        scratch_shapes=[
            pltpu.VMEM((g, dw), BF16),
            pltpu.VMEM((nt, ndp, m, rw), BF16),
            pltpu.VMEM((rw, ndp * g), BF16),
            pltpu.VMEM((nc, dw, WIDE), BF16),
            pltpu.VMEM((g, hid), BF16),
            pltpu.VMEM((g, hid), BF16),
            pltpu.VMEM((rw, hid), BF16),
            pltpu.VMEM((rw, hid), BF16),
            pltpu.VMEM((nc, ndp * g, WIDE), BF16),
            pltpu.VMEM((g, dw), BF16),
            pltpu.VMEM((nt, m, dw), BF16),
            dma((4,)), dma((nc,)), dma((2, nt)),
            dma((nt,)), dma((nt,)),
            dma((ndp,)), dma((ndp,)),
            dma((nt,)), dma((nt,)),
            dma((2, 2, nc)), dma((3, 2, nc)), dma((2, 2, nc)),
            dma((4, 2, nc)), dma((4, 2, nc)),
            dma((nt,)), dma((nt,)),
        ],
        compiler_params=pltpu.CompilerParams(
            collective_id=0, has_side_effects=True, vmem_limit_bytes=VMEM_BUDGET),
    )(*(pltpu.with_memory_space_constraint(x, pltpu.HBM)
        for x in (tokens, gate_weight, up_act, cotangent, moment1, moment2)))
    return pl.pallas_call(
        write_out,
        out_shape=tuple(pltpu.HBM(shape, dtype) for shape, dtype in results),
        in_specs=[vmem] * 5,
        out_specs=(any_spec,) * 5,
        scratch_shapes=[dma((5,))],
        compiler_params=pltpu.CompilerParams(vmem_limit_bytes=2**20),
    )(*(pltpu.with_memory_space_constraint(x, pltpu.VMEM) for x in held))


def write_out(*refs):
    sems = refs[-1]
    copies = [pltpu.make_async_copy(refs[i], refs[5 + i], sems.at[i]) for i in range(5)]
    for copy in reversed(copies):
        copy.start()
    for copy in copies:
        copy.wait()


def plain(ndp, nt, tokens, gate_weight, up_act, cotangent, moment1, moment2):
    gathered = lax.all_gather(tokens, "tensor", axis=0, tiled=True)
    gate_pre = jnp.dot(gathered, gate_weight, preferred_element_type=F32)
    up_grad, gate_grad = activation_grads(gate_pre, cotangent, up_act)
    term = lax.dot_general(
        gate_grad, gate_weight, (((1,), (1,)), ((), ())), preferred_element_type=F32).astype(BF16)
    in_grad = lax.psum_scatter(term, "tensor", scatter_dimension=0, tiled=True)
    partial_value = lax.dot_general(
        gathered, gate_grad, (((0,), (0,)), ((), ())), preferred_element_type=F32).astype(BF16)
    shard = lax.psum_scatter(partial_value.astype(F32), "dp", scatter_dimension=0, tiled=True)
    first, second, update = adam(shard * (1.0 / math.sqrt(ndp * gathered.shape[0])), moment1, moment2)
    return in_grad, up_grad, first.astype(BF16), second.astype(BF16), update


def local(ndp, nt, *args):
    (m, dw), (g, hid), rw = args[0].shape, args[2].shape, args[4].shape[0]
    need = (2 * dw * hid + 2 * ndp * g * (hid + 2 * rw) + 12 * g * hid + 16 * rw * hid + 16 * g * dw)
    fits = (need <= VMEM_BUDGET and ndp == CORES * CHIPS and nt > 1 and nt & (nt - 1) == 0
            and hid % WIDE == 0 and g % 128 == 0 and rw % 128 == 0 and m % 16 == 0
            and dw % (128 * (hid // WIDE)) == 0)
    return (fused if fits else plain)(ndp, nt, *args)


def solution(mesh):
    both = P("dp", "tensor")
    rows = P(("dp", "tensor"), None)
    return jax.shard_map(
        functools.partial(local, mesh.shape["dp"], mesh.shape["tensor"]),
        mesh=mesh,
        in_specs=(rows, P(None, "tensor"), both, both, both, both),
        out_specs=(rows, both, both, both, both),
        check_vma=False,
    )
```

time: 55.2 us -> 58.7 us (1.063)
  Pallas kernels: 54.4 us -> 57.7 us
    pallas_call x1, Pallas kernels: 52.2 us -> 55.5 us  [fused(): pl.pallas_call(functools.partial(kernel, ndp, nt), out_shape=tuple((pltpu...]
where the time goes in v1:
time: 58.7 us; the launch traced here: 58.3 us
  Pallas kernels  57.7 us (98%)
  between operations  0.64 us (1%)
    pallas_call x1, Pallas kernels, fused(): pl.pallas_call(functools.partial(kernel, ndp, nt), out_shape=tuple((pltpu...  55.5 us
    pallas_call x1, Pallas kernels, fused(): pl.pallas_call(write_out, out_shape=tuple((pltpu.HBM(shape, dtype) for sh...  2.24 us

profile of v1, /device:TPU:0, one launch (start us, length us, event | category | flops | bytes accessed | tf_op | source)
XLA Modules:
  0.0 58.3 jit_solution(16086229357925016503)
XLA Ops:
  0.6 55.5 %shard_map.101 = (bf16[32,2048]{1,0:T(8,128)(2,1)S(1)}, bf16[128,2048]{1,0:T(8,128)(2,1)S(1)}, bf16[256,2048]{1,0:T(8,128)(2,1)S(1)}, bf16[256,2048]{1,0:T(8,128)(2,1)S(1)}, f32[256,2048]{1,0:T(8,128)S(1)}) custom-call(bf16[32,2048]{1,0:T(8,128)(2,1)} %tok.1, bf16[2048,2048]{1,0:T(8,128)(2,1)} %w.1, bf16[128,2048]{1,0:T(8,128)(2,1)} %up.1, ...), custom_call_target="tpu_custom_call" | custom-call | tf_op jit(solution)/shard_map/pallas_call | solution.py:313
  56.1 2.2 %shard_map.102 = (bf16[32,2048]{1,0:T(8,128)(2,1)}, bf16[128,2048]{1,0:T(8,128)(2,1)}, bf16[256,2048]{1,0:T(8,128)(2,1)}, bf16[256,2048]{1,0:T(8,128)(2,1)}, f32[256,2048]{1,0:T(8,128)}) custom-call(bf16[32,2048]{1,0:T(8,128)(2,1)S(1)} %get-tuple-element.10.refs_0_, bf16[128,2048]{1,0:T(8,128)(2,1)S(1)} %get-tuple-element.11.refs_1_, ...), custom_call_target="tpu_custom_call" | custom-call | tf_op jit(solution)/shard_map/pallas_call | solution.py:342

commit v2 on v1

v2 whole, which is shorter than its diff:
```python
import functools
import math

import jax
import jax.numpy as jnp
from jax import lax
from jax.experimental import pallas as pl
from jax.experimental.pallas import tpu as pltpu
from jax.sharding import PartitionSpec as P

MESH = pl.DeviceIdType.MESH
F32, BF16 = jnp.float32, jnp.bfloat16
CORES = 2
CHIPS = 4
WIDE = 256
SUMMED = 4
LEAD = 4
W_DEPTH = 3
VMEM_BUDGET = 48 * 2**20


def adam(grad, moment1, moment2):
    first = 0.9 * moment1.astype(F32) + 0.1 * grad
    second = 0.95 * moment2.astype(F32) + 0.05 * grad * grad
    return first, second, first / (jnp.sqrt(second) + 1e-08)


def activation_grads(gate_pre, cot, up):
    sig = jax.nn.sigmoid(gate_pre)
    cot = cot.astype(F32)
    up_grad = (cot * gate_pre * sig).astype(BF16)
    gate_grad = (cot * up.astype(F32) * sig * (1.0 + gate_pre * (1.0 - sig))).astype(BF16)
    return up_grad, gate_grad


def phase(run):
    with jax.named_scope(run.__name__):
        run()


def flip(t, k):
    bit = 1
    while bit <= k:
        if k & bit:
            t = t + bit - 2 * bit * lax.rem(t // bit, 2)
        bit *= 2
    return t


def kernel(ndp, nt, tok, w, up, cot, m1, m2, in_grad, up_grad, nm1, nm2, upd,
           tg, xg, xp, xt, xtp, wv, upv, cotv, m1v, m2v, gall, term, termr, part_s, part_r,
           loc_sem, w_sem, cu_sem, tg_s, tg_r, x_s, x_r, xp_r, xf_sem, x2_s, x2_r, xp2_s, xp2_r,
           zs, zr, fs, ms, mr, rs, rr, ts, tr):
    d, t = lax.axis_index("dp"), lax.axis_index("tensor")
    z, core = d // CORES, lax.rem(d, CORES)
    mate = d + 1 - 2 * core
    m, dw = tok.shape
    g, hid = up.shape
    rw = m1.shape[0]
    nc, _, hc = wv.shape
    nr = part_s.shape[0]
    ng = nc - nr
    lead = min(LEAD, ng)
    scale = 1.0 / math.sqrt(ndp * g)

    half = z // 2
    near = z + 1 - 2 * lax.rem(z, 2)
    across = 2 - half
    far = 3 - 3 * half
    outer = lax.rem(z + half + 1, 2)
    chips = (near, across, far, z)
    NEAR, ACROSS, FAR, OWN = range(4)
    seen = ACROSS + outer
    first_rep = CORES * (1 - half)
    others = ndp - CORES
    beyond = others - CORES

    def inner_only(run):
        pl.when(outer == 0)(run)

    def outer_only(run):
        pl.when(outer == 1)(run)

    def rdma(src, dst, s, r, dp, tn):
        return pltpu.make_async_remote_copy(
            src_ref=src, dst_ref=dst, send_sem=s, recv_sem=r, device_id=(dp, tn), device_id_type=MESH)

    def rows_of(i, size):
        return pl.ds(pl.multiple_of(i * size, size), size)

    load_tok = pltpu.make_async_copy(tok, tg.at[0:m], loc_sem.at[0])
    load_x = pltpu.make_async_copy(tok.at[:, rows_of(d, rw)], xg.at[0, d], loc_sem.at[1])
    load_xp = pltpu.make_async_copy(
        tok.at[:, rows_of(near * CORES + core, rw)], xp.at[0, d - first_rep], loc_sem.at[4])
    load_m1 = pltpu.make_async_copy(m1, m1v, loc_sem.at[2])
    load_m2 = pltpu.make_async_copy(m2, m2v, loc_sem.at[3])

    def w_load(c):
        return pltpu.make_async_copy(w.at[:, rows_of(c, hc)], wv.at[c], w_sem.at[c])

    def cu_loads(k):
        src = rows_of(flip(t, k), m)
        dst = pl.ds(k * m, m)
        return (pltpu.make_async_copy(cot.at[src], cotv.at[dst], cu_sem.at[0, k]),
                pltpu.make_async_copy(up.at[src], upv.at[dst], cu_sem.at[1, k]))

    def tok_copy(k):
        return rdma(tg.at[0:m], tg.at[k * m:(k + 1) * m], tg_s.at[k], tg_r.at[k], d, flip(t, k))

    def features(chip, cr):
        return tg.at[0:m, rows_of(chip * CORES + cr, rw)]

    def x_near(cr):
        return rdma(features(near, cr), xg.at[0, d], x_s.at[cr], x_r.at[NEAR, core], near * CORES + cr, t)

    def x_across(cr):
        return rdma(features(across, cr), xg.at[0, d], x_s.at[2 + cr], x_r.at[seen, core],
                    across * CORES + cr, t)

    def xp_across(cr):
        return rdma(features(far, cr), xp.at[0, d - CORES * half], x_s.at[4 + cr], xp_r.at[seen, core],
                    across * CORES + cr, t)

    def x_mate():
        return rdma(features(z, 1 - core), xg.at[0, d], x_s.at[6], x_r.at[OWN, core], mate, t)

    def xp_mate():
        return rdma(features(near, 1 - core), xp.at[0, d - first_rep], x_s.at[7], xp_r.at[OWN, core], mate, t)

    def x_forward():
        return rdma(xp.at[0, pl.ds(first_rep, beyond)], xg.at[0, pl.ds(2 * first_rep, beyond)],
                    xf_sem.at[0], xf_sem.at[1], near * CORES + core, t)

    def xf_recv():
        return rdma(xp.at[0, 0:beyond], xg.at[0, pl.ds(CORES * CORES * (1 - half), beyond)],
                    xf_sem.at[0], xf_sem.at[1], near * CORES + core, t)

    def x_recv(origin, cr):
        return rdma(xg.at[0, d], xg.at[0, chips[origin] * CORES + cr], x_s.at[0], x_r.at[origin, cr], mate, t)

    def xp_recv(origin, cr):
        return rdma(xg.at[0, d], xp.at[0, chips[origin] * CORES + cr - first_rep], x_s.at[0],
                    xp_r.at[origin, cr], mate, t)

    def x2_copy(k):
        return rdma(xg.at[0], xg.at[k], x2_s.at[k], x2_r.at[k], d, flip(t, k))

    def xp2_copy(k):
        return rdma(xp.at[0], xp.at[k], xp2_s.at[k], xp2_r.at[k], d, flip(t, k))

    def term_copy(k):
        return rdma(term.at[k * m:(k + 1) * m], termr.at[k], ts.at[k], tr.at[k], d, flip(t, k))

    def block(c, part, chip, cr):
        start = pl.multiple_of((chip * CORES + cr) * g, g) + (m if part else 0)
        return gall.at[c, pl.ds(pl.multiple_of(start, m), g - m if part else m)]

    def own_copy(c, part, to):
        b = block(c, part, z, core)
        if to == NEAR:
            return rdma(b, b, zs.at[0, part, c], zr.at[NEAR, part, c], near * CORES + core, t)
        return rdma(b, b, zs.at[1, part, c], zr.at[seen, part, c], across * CORES + core, t)

    def arrival(c, part, origin):
        b = block(c, part, chips[origin], core)
        return rdma(b, b, zs.at[0, part, c], zr.at[origin, part, c], near * CORES + core, t)

    def forward_copy(c, part, origin):
        b = block(c, part, chips[origin], core)
        return rdma(b, b, fs.at[origin - 1, part, c], zr.at[origin, part, c], near * CORES + core, t)

    def mate_copy(c, part, origin):
        b = block(c, part, chips[origin], core)
        return rdma(b, b, ms.at[origin, part, c], mr.at[origin, part, c], mate, t)

    def mate_recv(c, part, origin):
        b = block(c, part, chips[origin], 1 - core)
        return rdma(b, b, ms.at[origin, part, c], mr.at[origin, part, c], mate, t)

    def part_copy(j):
        return rdma(part_s.at[j], part_r.at[j], rs.at[j], rr.at[j], near * CORES + core, t)

    def take(c, part, origin, pass_on=True):
        arrival(c, part, origin).wait_recv()
        if origin != NEAR and pass_on:
            @inner_only
            def _():
                forward_copy(c, part, origin).start()
        mate_copy(c, part, origin).start()

    def grads(c, part):
        here = slice(m, g) if part else slice(0, m)
        cols = rows_of(c, hc)
        gate_pre = jnp.dot(tg[here], wv[c], preferred_element_type=F32)
        ug, gg = activation_grads(gate_pre, cotv[here, cols], upv[here, cols])
        start = pl.multiple_of(d * g, g) + (m if part else 0)
        gall[c, pl.ds(pl.multiple_of(start, m), g - m if part else m), :] = gg
        for k in range(1, nt) if part else (0,):
            low = (k - 1) * m if part else 0
            up_grad[rows_of(flip(t, k), m), cols] = ug[low:low + m]

    def near_copies(c, run):
        pl.when(jnp.logical_or(outer == 1, c < ng))(run)

    def send_own(c, part):
        own_copy(c, part, ACROSS).start()

        def to_near():
            own_copy(c, part, NEAR).start()
        near_copies(c, to_near)
        mate_copy(c, part, OWN).start()

    span = dw // nc

    def term_part(n):
        rows = rows_of(n, span)
        own = rows_of(d, g)
        total = jnp.zeros((g, span), F32)
        for c in range(nc):
            total += lax.dot_general(
                gall[c, own, :], wv[c, rows, :], (((1,), (1,)), ((), ())), preferred_element_type=F32)
        term[:, rows] = total.astype(BF16)

    def mates_wait(c, origins):
        for origin in origins:
            for part in range(2):
                mate_recv(c, part, origin).wait_recv()

    def step(c, grad):
        cols = rows_of(c, hc)
        first, second, change = adam(grad * scale, m1v[:, cols], m2v[:, cols])
        nm1[:, cols] = first.astype(BF16)
        nm2[:, cols] = second.astype(BF16)
        upd[:, cols] = change

    def update(c, origins=(OWN, NEAR, ACROSS, FAR)):
        mates_wait(c, origins)
        step(c, jnp.dot(xt[...], gall[c], preferred_element_type=F32))

    def reduce(c, j):
        mates_wait(c, (OWN, ACROSS, FAR))
        rows = pl.ds(pl.multiple_of(first_rep * g, g), others * g)
        part_s[j] = jnp.dot(xtp[...], gall[c, rows, :], preferred_element_type=F32).astype(BF16)
        part_copy(j).start()

    def finish(c, j):
        mates_wait(c, (OWN,))
        own = rows_of(z, CORES * g)
        grad = jnp.dot(xt[:, own], gall[c, own, :], preferred_element_type=F32)
        part_copy(j).wait_recv()
        step(c, grad + part_r[j].astype(F32))

    depth = min(W_DEPTH, nc)

    load_tok.start()
    for copy in cu_loads(0):
        copy.start()
    for c in range(depth):
        w_load(c).start()

    barrier = pltpu.get_barrier_semaphore()

    def greet(dp, tn):
        pl.semaphore_signal(barrier, inc=1, device_id=(dp, tn), device_id_type=MESH)

    for k in range(1, nt):
        greet(d, flip(t, k))
    greet(mate, t)
    for cr in range(CORES):
        greet(near * CORES + cr, t)

    @inner_only
    def _():
        for chip in (across, far):
            for cr in range(CORES):
                greet(chip * CORES + cr, t)

    @phase
    def tok_load():
        load_tok.wait()

    @phase
    def meet():
        pl.semaphore_wait(barrier, nt - 1 + 1 + 2 * CORES)

    for k in range(1, nt):
        tok_copy(k).start()

    @phase
    def own_loads():
        for copy in cu_loads(0):
            copy.wait()

    @phase
    def own_grads():
        @pl.loop(0, nc)
        def _(c):
            w_load(c).wait()

            @pl.when(c + depth < nc)
            def _():
                w_load(c + depth).start()
            grads(c, 0)

            @pl.when(c > 0)
            def _():
                send_own(c - 1, 0)

    for k in range(1, nt):
        for copy in cu_loads(k):
            copy.start()
    load_x.start()
    inner_only(load_xp.start)
    load_m1.start()
    load_m2.start()
    send_own(nc - 1, 0)
    for cr in range(CORES):
        xp_across(cr).start()
    for cr in range(CORES):
        x_across(cr).start()
        x_near(cr).start()
    x_mate().start()
    inner_only(lambda: xp_mate().start())

    @phase
    def inner_forwards():
        @inner_only
        def _():
            @pl.loop(0, ng)
            def _(c):
                take(c, 0, ACROSS)
                take(c, 0, FAR)

    @phase
    def tok_wait():
        for k in range(1, nt):
            for copy in cu_loads(k):
                copy.wait()
        for k in range(1, nt):
            tok_copy(k).wait_recv()

    @phase
    def other_grads():
        @pl.loop(0, nc)
        def _(c):
            grads(c, 1)

            @pl.when(c > 0)
            def _():
                send_own(c - 1, 1)

    @phase
    def x_exchange():
        term_part(0)
        send_own(nc - 1, 1)
        load_x.wait()
        x_recv(OWN, 1 - core).wait_recv()
        for cr in range(CORES):
            x_recv(NEAR, cr).wait_recv()

        @inner_only
        def _():
            for origin in (ACROSS, FAR):
                for cr in range(CORES):
                    xp_recv(origin, cr).wait_recv()
            x_forward().start()
            load_xp.wait()
            xp_recv(OWN, 1 - core).wait_recv()
            for origin in (ACROSS, FAR):
                for cr in range(CORES):
                    x_recv(origin, cr).wait_recv()
            for k in range(1, nt):
                x2_copy(k).start()
            for k in range(1, nt):
                xp2_copy(k).start()

    @phase
    def terms():
        @pl.loop(1, nc)
        def _(n):
            term_part(n)

    @phase
    def outer_takes():
        @outer_only
        def _():
            xf_recv().wait_recv()
            for k in range(1, nt):
                x2_copy(k).start()

            @pl.loop(0, ng)
            def _(c):
                take(c, 0, ACROSS)
                take(c, 0, FAR)

    for k in range(1, nt):
        term_copy(k).start()

    @phase
    def near_takes():
        @pl.loop(0, ng)
        def _(c):
            take(c, 0, NEAR)

        @inner_only
        def _():
            @pl.loop(ng, nc)
            def _(c):
                for origin in (NEAR, ACROSS, FAR):
                    take(c, 0, origin, False)

    def takes(c):
        @phase
        def others_in():
            for origin in (NEAR, ACROSS, FAR):
                take(c, 1, origin)

    @pl.loop(0, lead)
    def _(c):
        takes(c)

    @phase
    def x_wait():
        for k in range(1, nt):
            x2_copy(k).wait_recv()

    load_m1.wait()
    load_m2.wait()

    @phase
    def transposes():
        for i in range(ndp):
            xt[:, i * g:(i + 1) * g] = xg[:, i].reshape(g, rw).T

    @pl.loop(lead, ng)
    def _(c):
        takes(c)

        @phase
        def updates():
            update(c - lead)

    def input_grads():
        with jax.named_scope("input_grads"):
            total = term[0:m, :].astype(F32)
            for k in range(1, nt):
                term_copy(k).wait_recv()
                total += termr[k].astype(F32)
            in_grad[...] = total.astype(BF16)

    @inner_only
    def _():
        @phase
        def xp_wait():
            for k in range(1, nt):
                xp2_copy(k).wait_recv()
            for i in range(others):
                xtp[:, i * g:(i + 1) * g] = xp[:, i].reshape(g, rw).T

        for j in range(nr):
            @phase
            def last_in():
                for origin in (ACROSS, FAR, NEAR):
                    take(ng + j, 1, origin, False)

            @phase
            def updates():
                update(ng - lead + j)

            @phase
            def reduces():
                reduce(ng + j, j)

        @pl.loop(ng - lead + nr, ng)
        def _(c):
            update(c)

        @pl.loop(ng, nc)
        def _(c):
            update(c, (NEAR,))
        input_grads()

    @outer_only
    def _():
        @pl.loop(ng - lead, ng)
        def _(c):
            @phase
            def updates():
                update(c)
        input_grads()
        for j in range(nr):
            @phase
            def finishes():
                finish(ng + j, j)

    @phase
    def drain():
        for k in range(1, nt):
            tok_copy(k).wait_send()
            x2_copy(k).wait_send()
            term_copy(k).wait_send()
        for cr in range(CORES):
            x_near(cr).wait_send()
            x_across(cr).wait_send()
            xp_across(cr).wait_send()
        x_mate().wait_send()

        @pl.loop(0, nc)
        def _(c):
            for p in range(2):
                own_copy(c, p, ACROSS).wait_send()
                near_copies(c, own_copy(c, p, NEAR).wait_send)
                mate_copy(c, p, OWN).wait_send()

        @pl.loop(0, ng)
        def _(c):
            for p in range(2):
                for origin in (NEAR, ACROSS, FAR):
                    mate_copy(c, p, origin).wait_send()

        @inner_only
        def _():
            xp_mate().wait_send()
            x_forward().wait_send()
            for k in range(1, nt):
                xp2_copy(k).wait_send()

            @pl.loop(0, ng)
            def _(c):
                for p in range(2):
                    forward_copy(c, p, ACROSS).wait_send()
                    forward_copy(c, p, FAR).wait_send()

            @pl.loop(ng, nc)
            def _(c):
                for p in range(2):
                    for origin in (NEAR, ACROSS, FAR):
                        mate_copy(c, p, origin).wait_send()
            for j in range(nr):
                part_copy(j).wait_send()


def fused(ndp, nt, tokens, gate_weight, up_act, cotangent, moment1, moment2):
    m, dw = tokens.shape
    g, hid = up_act.shape
    rw = moment1.shape[0]
    nc = hid // WIDE
    nr = nc // SUMMED
    any_spec, vmem = pl.BlockSpec(memory_space=pltpu.HBM), pl.BlockSpec(memory_space=pltpu.VMEM)
    dma = pltpu.SemaphoreType.DMA
    results = (((m, dw), BF16), ((g, hid), BF16), ((rw, hid), BF16), ((rw, hid), BF16), ((rw, hid), F32))
    held = pl.pallas_call(
        functools.partial(kernel, ndp, nt),
        out_shape=tuple(pltpu.VMEM(shape, dtype) for shape, dtype in results),
        in_specs=[any_spec] * 6,
        out_specs=(vmem,) * 5,
        scratch_shapes=[
            pltpu.VMEM((g, dw), BF16),
            pltpu.VMEM((nt, ndp, m, rw), BF16),
            pltpu.VMEM((nt, ndp - CORES, m, rw), BF16),
            pltpu.VMEM((rw, ndp * g), BF16),
            pltpu.VMEM((rw, (ndp - CORES) * g), BF16),
            pltpu.VMEM((nc, dw, WIDE), BF16),
            pltpu.VMEM((g, hid), BF16),
            pltpu.VMEM((g, hid), BF16),
            pltpu.VMEM((rw, hid), BF16),
            pltpu.VMEM((rw, hid), BF16),
            pltpu.VMEM((nc, ndp * g, WIDE), BF16),
            pltpu.VMEM((g, dw), BF16),
            pltpu.VMEM((nt, m, dw), BF16),
            pltpu.VMEM((nr, rw, WIDE), BF16),
            pltpu.VMEM((nr, rw, WIDE), BF16),
            dma((5,)), dma((nc,)), dma((2, nt)),
            dma((nt,)), dma((nt,)),
            dma((8,)), dma((4, CORES)), dma((4, CORES)), dma((2,)),
            dma((nt,)), dma((nt,)), dma((nt,)), dma((nt,)),
            dma((2, 2, nc)), dma((3, 2, nc)), dma((2, 2, nc)),
            dma((4, 2, nc)), dma((4, 2, nc)),
            dma((nr,)), dma((nr,)),
            dma((nt,)), dma((nt,)),
        ],
        compiler_params=pltpu.CompilerParams(
            collective_id=0, has_side_effects=True, vmem_limit_bytes=VMEM_BUDGET),
    )(*(pltpu.with_memory_space_constraint(x, pltpu.HBM)
        for x in (tokens, gate_weight, up_act, cotangent, moment1, moment2)))
    return pl.pallas_call(
        write_out,
        out_shape=tuple(pltpu.HBM(shape, dtype) for shape, dtype in results),
        in_specs=[vmem] * 5,
        out_specs=(any_spec,) * 5,
        scratch_shapes=[dma((5,))],
        compiler_params=pltpu.CompilerParams(vmem_limit_bytes=2**20),
    )(*(pltpu.with_memory_space_constraint(x, pltpu.VMEM) for x in held))


def write_out(*refs):
    sems = refs[-1]
    copies = [pltpu.make_async_copy(refs[i], refs[5 + i], sems.at[i]) for i in range(5)]
    for copy in reversed(copies):
        copy.start()
    for copy in copies:
        copy.wait()


def plain(ndp, nt, tokens, gate_weight, up_act, cotangent, moment1, moment2):
    gathered = lax.all_gather(tokens, "tensor", axis=0, tiled=True)
    gate_pre = jnp.dot(gathered, gate_weight, preferred_element_type=F32)
    up_grad, gate_grad = activation_grads(gate_pre, cotangent, up_act)
    term = lax.dot_general(
        gate_grad, gate_weight, (((1,), (1,)), ((), ())), preferred_element_type=F32).astype(BF16)
    in_grad = lax.psum_scatter(term, "tensor", scatter_dimension=0, tiled=True)
    partial_value = lax.dot_general(
        gathered, gate_grad, (((0,), (0,)), ((), ())), preferred_element_type=F32).astype(BF16)
    shard = lax.psum_scatter(partial_value.astype(F32), "dp", scatter_dimension=0, tiled=True)
    first, second, update = adam(shard * (1.0 / math.sqrt(ndp * gathered.shape[0])), moment1, moment2)
    return in_grad, up_grad, first.astype(BF16), second.astype(BF16), update


def local(ndp, nt, *args):
    (m, dw), (g, hid), rw = args[0].shape, args[2].shape, args[4].shape[0]
    need = (2 * dw * hid + 2 * ndp * g * (hid + 2 * rw) + 12 * g * hid + 16 * rw * hid + 16 * g * dw)
    fits = (need <= VMEM_BUDGET and hid >= 8 * WIDE and ndp == CORES * CHIPS and nt > 1 and nt & (nt - 1) == 0
            and hid % WIDE == 0 and g % 128 == 0 and rw % 128 == 0 and m % 16 == 0
            and dw % (128 * (hid // WIDE)) == 0)
    return (fused if fits else plain)(ndp, nt, *args)


def solution(mesh):
    both = P("dp", "tensor")
    rows = P(("dp", "tensor"), None)
    return jax.shard_map(
        functools.partial(local, mesh.shape["dp"], mesh.shape["tensor"]),
        mesh=mesh,
        in_specs=(rows, P(None, "tensor"), both, both, both, both),
        out_specs=(rows, both, both, both, both),
        check_vma=False,
    )
```

time: 58.7 us -> 47.9 us (0.82)
  Pallas kernels: 57.7 us -> 47 us
    pallas_call x1, Pallas kernels: 55.5 us -> 44.8 us  [fused(): pl.pallas_call(functools.partial(kernel, ndp, nt), out_shape=tuple((pltpu...]
where the time goes in v2:
time: 47.9 us; the launch traced here: 47.7 us
  Pallas kernels  47 us (98%)
  between operations  0.64 us (1%)
    pallas_call x1, Pallas kernels, fused(): pl.pallas_call(functools.partial(kernel, ndp, nt), out_shape=tuple((pltpu...  44.8 us
    pallas_call x1, Pallas kernels, fused(): pl.pallas_call(write_out, out_shape=tuple((pltpu.HBM(shape, dtype) for sh...  2.24 us

profile of v2, /device:TPU:0, one launch (start us, length us, event | category | flops | bytes accessed | tf_op | source)
XLA Modules:
  0.0 47.7 jit_solution(12261535163185355703)
XLA Ops:
  0.6 44.8 %shard_map.101 = (bf16[32,2048]{1,0:T(8,128)(2,1)S(1)}, bf16[128,2048]{1,0:T(8,128)(2,1)S(1)}, bf16[256,2048]{1,0:T(8,128)(2,1)S(1)}, bf16[256,2048]{1,0:T(8,128)(2,1)S(1)}, f32[256,2048]{1,0:T(8,128)S(1)}) custom-call(bf16[32,2048]{1,0:T(8,128)(2,1)} %tok.1, bf16[2048,2048]{1,0:T(8,128)(2,1)} %w.1, bf16[128,2048]{1,0:T(8,128)(2,1)} %up.1, ...), custom_call_target="tpu_custom_call" | custom-call | tf_op jit(solution)/shard_map/pallas_call | solution.py:552
  45.4 2.2 %shard_map.102 = (bf16[32,2048]{1,0:T(8,128)(2,1)}, bf16[128,2048]{1,0:T(8,128)(2,1)}, bf16[256,2048]{1,0:T(8,128)(2,1)}, bf16[256,2048]{1,0:T(8,128)(2,1)}, f32[256,2048]{1,0:T(8,128)}) custom-call(bf16[32,2048]{1,0:T(8,128)(2,1)S(1)} %get-tuple-element.10.refs_0_, bf16[128,2048]{1,0:T(8,128)(2,1)S(1)} %get-tuple-element.11.refs_1_, ...), custom_call_target="tpu_custom_call" | custom-call | tf_op jit(solution)/shard_map/pallas_call | solution.py:586

commit v3 on v2

v3 whole, which is shorter than its diff:
```python
import functools
import math

import jax
import jax.numpy as jnp
from jax import lax
from jax.experimental import pallas as pl
from jax.experimental.pallas import tpu as pltpu
from jax.sharding import PartitionSpec as P

MESH = pl.DeviceIdType.MESH
F32, BF16 = jnp.float32, jnp.bfloat16
CORES = 2
CHIPS = 4
WIDE = 256
SUMMED = 2
LEAD = 4
W_DEPTH = 3
VMEM_BUDGET = 48 * 2**20


def adam(grad, moment1, moment2):
    first = 0.9 * moment1.astype(F32) + 0.1 * grad
    second = 0.95 * moment2.astype(F32) + 0.05 * grad * grad
    return first, second, first / (jnp.sqrt(second) + 1e-08)


def activation_grads(gate_pre, cot, up):
    sig = jax.nn.sigmoid(gate_pre)
    cot = cot.astype(F32)
    up_grad = (cot * gate_pre * sig).astype(BF16)
    gate_grad = (cot * up.astype(F32) * sig * (1.0 + gate_pre * (1.0 - sig))).astype(BF16)
    return up_grad, gate_grad


def phase(run):
    with jax.named_scope(run.__name__):
        run()


def flip(t, k):
    bit = 1
    while bit <= k:
        if k & bit:
            t = t + bit - 2 * bit * lax.rem(t // bit, 2)
        bit *= 2
    return t


def kernel(ndp, nt, tok, w, up, cot, m1, m2, in_grad, up_grad, nm1, nm2, upd,
           tg, xg, xp, xt, xtp, wv, upv, cotv, m1v, m2v, gall, term, termr, part_s, part_r,
           loc_sem, w_sem, cu_sem, tok_sem, x_sem, x2_sem, zs, fs, ms, zr_near, zr_rest,
           mr_near, mr_rest, rs, rr, term_sem):
    d, t = lax.axis_index("dp"), lax.axis_index("tensor")
    z, core = d // CORES, lax.rem(d, CORES)
    mate = d + 1 - 2 * core
    m, dw = tok.shape
    g, hid = up.shape
    rw = m1.shape[0]
    nc, _, hc = wv.shape
    nr = part_s.shape[0]
    ng = nc - nr
    lead = min(LEAD, ng)
    scale = 1.0 / math.sqrt(ndp * g)

    half = z // 2
    near = z + 1 - 2 * lax.rem(z, 2)
    across = 2 - half
    far = 3 - 3 * half
    outer = lax.rem(z + half + 1, 2)
    first_rep = CORES * (1 - half)
    others = ndp - CORES
    beyond = others - CORES

    def inner_only(run):
        pl.when(outer == 0)(run)

    def outer_only(run):
        pl.when(outer == 1)(run)

    def rdma(src, dst, s, r, dp, tn):
        return pltpu.make_async_remote_copy(
            src_ref=src, dst_ref=dst, send_sem=s, recv_sem=r, device_id=(dp, tn), device_id_type=MESH)

    def rows_of(i, size):
        return pl.ds(pl.multiple_of(i * size, size), size)

    served = near * CORES + 1 - core

    load_tok = pltpu.make_async_copy(tok, tg.at[0:m], loc_sem.at[0])
    load_x = pltpu.make_async_copy(tok.at[:, rows_of(d, rw)], xg.at[0, d], loc_sem.at[1])
    load_xp = pltpu.make_async_copy(tok.at[:, rows_of(served, rw)], xp.at[0, d - first_rep], loc_sem.at[4])
    load_m1 = pltpu.make_async_copy(m1, m1v, loc_sem.at[2])
    load_m2 = pltpu.make_async_copy(m2, m2v, loc_sem.at[3])

    def w_load(c):
        return pltpu.make_async_copy(w.at[:, rows_of(c, hc)], wv.at[c], w_sem.at[c])

    def cu_loads(k):
        src = rows_of(flip(t, k), m)
        dst = pl.ds(k * m, m)
        return (pltpu.make_async_copy(cot.at[src], cotv.at[dst], cu_sem.at[1 if k else 0]),
                pltpu.make_async_copy(up.at[src], upv.at[dst], cu_sem.at[2 if k else 0]))

    def cu_wait(first):
        if first:
            pltpu.make_async_copy(cot.at[0:2 * m], cotv.at[0:2 * m], cu_sem.at[0]).wait()
        else:
            pltpu.make_async_copy(cot.at[m:g], cotv.at[m:g], cu_sem.at[1]).wait()
            pltpu.make_async_copy(up.at[m:g], upv.at[m:g], cu_sem.at[2]).wait()

    def tok_copy(k):
        return rdma(tg.at[0:m], tg.at[k * m:(k + 1) * m], tok_sem.at[0], tok_sem.at[1], d, flip(t, k))

    tok_all = rdma(tg.at[m:g], tg.at[m:g], tok_sem.at[0], tok_sem.at[1], mate, t)

    def features(chip, cr):
        return tg.at[0:m, rows_of(chip * CORES + cr, rw)]

    def x_near(cr):
        return rdma(features(near, cr), xg.at[0, d], x_sem.at[0], x_sem.at[1], near * CORES + cr, t)

    def x_across(cr):
        return rdma(features(across, cr), xg.at[0, d], x_sem.at[0], x_sem.at[1], across * CORES + cr, t)

    def xp_across(cr):
        return rdma(features(far, 1 - cr), xp.at[0, d - CORES * half], x_sem.at[0], x_sem.at[2],
                    across * CORES + cr, t)

    x_mate = rdma(features(z, 1 - core), xg.at[0, d], x_sem.at[0], x_sem.at[1], mate, t)
    xp_mate = rdma(features(near, core), xp.at[0, d - first_rep], x_sem.at[3], x_sem.at[4], mate, t)
    x_forward = rdma(xp.at[0, pl.ds(first_rep, beyond)], xg.at[0, pl.ds(CORES * first_rep, beyond)],
                     x_sem.at[5], x_sem.at[1], served, t)
    x_all = rdma(xg.at[0, 0:ndp - 1], xg.at[0, 0:ndp - 1], x_sem.at[0], x_sem.at[1], mate, t)
    xp_beyond = rdma(xp.at[0, 0:beyond], xp.at[0, 0:beyond], x_sem.at[5], x_sem.at[2], mate, t)

    def x2_copy(k):
        return rdma(xg.at[0], xg.at[k], x2_sem.at[0], x2_sem.at[1], d, flip(t, k))

    def xp2_copy(k):
        return rdma(xp.at[0], xp.at[k], x2_sem.at[2], x2_sem.at[3], d, flip(t, k))

    x2_all = rdma(xg.at[1:nt], xg.at[1:nt], x2_sem.at[0], x2_sem.at[1], mate, t)
    xp2_all = rdma(xp.at[1:nt], xp.at[1:nt], x2_sem.at[2], x2_sem.at[3], mate, t)

    def term_copy(k):
        return rdma(term.at[k * m:(k + 1) * m], termr.at[k], term_sem.at[0], term_sem.at[1], d, flip(t, k))

    term_out = rdma(term.at[m:g], term.at[m:g], term_sem.at[0], term_sem.at[1], mate, t)
    term_in = rdma(termr.at[1:nt], termr.at[1:nt], term_sem.at[0], term_sem.at[1], mate, t)

    def replica(c, chip, cr):
        return gall.at[c, rows_of(chip * CORES + cr, g)]

    def block(c, part, chip, cr):
        start = pl.multiple_of((chip * CORES + cr) * g, g) + (m if part else 0)
        return gall.at[c, pl.ds(pl.multiple_of(start, m), g - m if part else m)]

    def to_near(c, part):
        b = block(c, part, z, core)
        return rdma(b, b, zs.at[0], zr_near.at[c], near * CORES + core, t)

    def to_across(c, part):
        b = block(c, part, z, core)
        return rdma(b, b, zs.at[1], zr_rest.at[part, c], across * CORES + core, t)

    def near_in(c):
        b = replica(c, near, core)
        rdma(b, b, zs.at[0], zr_near.at[c], near * CORES + core, t).wait_recv()

    def rest_in(c, part):
        b = gall.at[c, 0:2 * (g - m if part else m)]
        rdma(b, b, zs.at[0], zr_rest.at[part, c], near * CORES + core, t).wait_recv()

    def forward(c, part):
        for chip in (across, far):
            b = block(c, part, chip, core)
            rdma(b, b, fs.at[0], zr_rest.at[part, c], near * CORES + core, t).start()

    def mate_copy(c, chip):
        b = replica(c, chip, core)
        if chip is near:
            return rdma(b, b, ms.at[1], mr_near.at[c], mate, t)
        return rdma(b, b, ms.at[0 if chip is z else 1], mr_rest.at[c], mate, t)

    def mate_near_in(c):
        b = gall.at[c, 0:g]
        rdma(b, b, ms.at[0], mr_near.at[c], mate, t).wait_recv()

    def mate_rest_in(c, replicas):
        b = gall.at[c, 0:replicas * g]
        rdma(b, b, ms.at[0], mr_rest.at[c], mate, t).wait_recv()

    def part_copy(j):
        return rdma(part_s.at[j], part_r.at[j], rs.at[0], rr.at[j], served, t)

    def grads(c, part):
        here = slice(m, g) if part else slice(0, m)
        cols = rows_of(c, hc)
        gate_pre = jnp.dot(tg[here], wv[c], preferred_element_type=F32)
        ug, gg = activation_grads(gate_pre, cotv[here, cols], upv[here, cols])
        start = pl.multiple_of(d * g, g) + (m if part else 0)
        gall[c, pl.ds(pl.multiple_of(start, m), g - m if part else m), :] = gg
        for k in range(1, nt) if part else (0,):
            low = (k - 1) * m if part else 0
            up_grad[rows_of(flip(t, k), m), cols] = ug[low:low + m]

    def send_own(c, part):
        to_across(c, part).start()

        @pl.when(jnp.logical_or(outer == 1, c < ng))
        def _():
            to_near(c, part).start()
        if part:
            mate_copy(c, z).start()

    span = dw // nc

    def term_part(n):
        rows = rows_of(n, span)
        own = rows_of(d, g)
        total = jnp.zeros((g, span), F32)
        for c in range(nc):
            total += lax.dot_general(
                gall[c, own, :], wv[c, rows, :], (((1,), (1,)), ((), ())), preferred_element_type=F32)
        term[:, rows] = total.astype(BF16)

    def step(c, grad):
        cols = rows_of(c, hc)
        first, second, change = adam(grad * scale, m1v[:, cols], m2v[:, cols])
        nm1[:, cols] = first.astype(BF16)
        nm2[:, cols] = second.astype(BF16)
        upd[:, cols] = change

    def update(c, reduced=False):
        mate_near_in(c)
        if not reduced:
            mate_rest_in(c, 3)
        step(c, jnp.dot(xt[...], gall[c], preferred_element_type=F32))

    def reduce(c, j):
        mate_rest_in(c, 3)
        rows = pl.ds(pl.multiple_of(first_rep * g, g), others * g)
        part_s[j] = jnp.dot(xtp[...], gall[c, rows, :], preferred_element_type=F32).astype(BF16)
        part_copy(j).start()

    def finish(c, j):
        mate_rest_in(c, 1)
        own = rows_of(z, CORES * g)
        grad = jnp.dot(xt[:, own], gall[c, own, :], preferred_element_type=F32)
        part_copy(j).wait_recv()
        step(c, grad + part_r[j].astype(F32))

    depth = min(W_DEPTH, nc)

    load_tok.start()
    barrier = pltpu.get_barrier_semaphore()

    def greet(dp, tn):
        pl.semaphore_signal(barrier, inc=1, device_id=(dp, tn), device_id_type=MESH)

    for k in range(1, nt):
        greet(d, flip(t, k))
    greet(mate, t)
    for cr in range(CORES):
        greet(near * CORES + cr, t)

    @inner_only
    def _():
        for chip in (across, far):
            for cr in range(CORES):
                greet(chip * CORES + cr, t)

    @phase
    def tok_load():
        load_tok.wait()

    for copy in cu_loads(0):
        copy.start()
    for c in range(depth):
        w_load(c).start()

    @phase
    def meet():
        pl.semaphore_wait(barrier, nt - 1 + 1 + 2 * CORES)

    for k in range(1, nt):
        tok_copy(k).start()

    @phase
    def own_loads():
        cu_wait(True)

    @phase
    def own_grads():
        @pl.loop(0, nc)
        def _(c):
            w_load(c).wait()

            @pl.when(c + depth < nc)
            def _():
                w_load(c + depth).start()
            grads(c, 0)

            @pl.when(jnp.logical_and(c > 0, c <= ng))
            def _():
                send_own(c - 1, 0)

    for k in range(1, nt):
        for copy in cu_loads(k):
            copy.start()
    load_x.start()
    inner_only(load_xp.start)
    load_m1.start()
    load_m2.start()
    for cr in range(CORES):
        xp_across(cr).start()
    for cr in range(CORES):
        x_across(cr).start()
        x_near(cr).start()
    x_mate.start()
    inner_only(xp_mate.start)

    @pl.loop(ng, nc)
    def _(c):
        send_own(c, 0)

    @phase
    def inner_forwards():
        @inner_only
        def _():
            @pl.loop(0, ng)
            def _(c):
                rest_in(c, 0)
                forward(c, 0)

    @phase
    def tok_wait():
        cu_wait(False)
        tok_all.wait_recv()

    @phase
    def other_grads():
        @pl.loop(0, nc)
        def _(c):
            grads(c, 1)

            @pl.when(c > 0)
            def _():
                send_own(c - 1, 1)

    @phase
    def x_exchange():
        term_part(0)
        send_own(nc - 1, 1)
        load_x.wait()

        @inner_only
        def _():
            xp_beyond.wait_recv()
            x_forward.start()
            load_xp.wait()
            xp_mate.wait_recv()
            x_all.wait_recv()
            for k in range(1, nt):
                x2_copy(k).start()
            for k in range(1, nt):
                xp2_copy(k).start()

    @phase
    def terms():
        @pl.loop(1, nc)
        def _(n):
            term_part(n)

    @phase
    def outer_x():
        @outer_only
        def _():
            x_all.wait_recv()
            for k in range(1, nt):
                x2_copy(k).start()
            for k in range(1, nt):
                term_copy(k).start()

    def takes(c):
        @phase
        def others_in():
            near_in(c)
            mate_copy(c, near).start()

            @outer_only
            def _():
                rest_in(c, 0)
            rest_in(c, 1)

            @inner_only
            def _():
                forward(c, 1)
            mate_copy(c, across).start()
            mate_copy(c, far).start()

    @pl.loop(0, lead)
    def _(c):
        takes(c)

    @inner_only
    def _():
        for k in range(1, nt):
            term_copy(k).start()

    @phase
    def x_wait():
        x2_all.wait_recv()

    load_m1.wait()
    load_m2.wait()

    @phase
    def transposes():
        for i in range(ndp):
            xt[:, i * g:(i + 1) * g] = xg[:, i].reshape(g, rw).T

    @pl.loop(lead, ng)
    def _(c):
        takes(c)

        @phase
        def updates():
            update(c - lead)

    def input_grads():
        with jax.named_scope("input_grads"):
            total = term[0:m, :].astype(F32)
            term_in.wait_recv()
            for k in range(1, nt):
                total += termr[k].astype(F32)
            in_grad[...] = total.astype(BF16)

    @inner_only
    def _():
        @phase
        def xp_wait():
            xp2_all.wait_recv()
            for i in range(others):
                xtp[:, i * g:(i + 1) * g] = xp[:, i].reshape(g, rw).T

        for j in range(nr):
            @phase
            def last_in():
                rest_in(ng + j, 0)
                rest_in(ng + j, 1)
                mate_copy(ng + j, across).start()
                mate_copy(ng + j, far).start()

            @phase
            def updates():
                update(ng - lead + j)

            @phase
            def reduces():
                reduce(ng + j, j)

            @phase
            def near_last():
                near_in(ng + j)
                mate_copy(ng + j, near).start()

        @pl.loop(ng - lead + nr, ng)
        def _(c):
            update(c)

        @pl.loop(ng, nc)
        def _(c):
            update(c, True)
        input_grads()

    @outer_only
    def _():
        @pl.loop(ng - lead, ng)
        def _(c):
            @phase
            def updates():
                update(c)
        input_grads()
        for j in range(nr):
            @phase
            def finishes():
                finish(ng + j, j)

    def sent(sem, chunks, replicas):
        b = gall.at[0:chunks, 0:replicas * g]
        rdma(b, b, sem, sem, mate, t).wait_send()

    @phase
    def drain():
        tok_all.wait_send()
        x2_all.wait_send()
        term_out.wait_send()
        x_all.wait_send()
        sent(zs.at[1], nc, 1)
        sent(ms.at[0], nc, 1)

        @outer_only
        def _():
            sent(zs.at[0], nc, 1)
            sent(ms.at[1], ng, 3)

        @inner_only
        def _():
            sent(zs.at[0], ng, 1)
            sent(ms.at[1], nc, 3)
            sent(fs.at[0], ng, 2)
            xp_mate.wait_send()
            x_forward.wait_send()
            xp2_all.wait_send()
            rdma(part_s, part_s, rs.at[0], rs.at[0], mate, t).wait_send()


def fused(ndp, nt, tokens, gate_weight, up_act, cotangent, moment1, moment2):
    m, dw = tokens.shape
    g, hid = up_act.shape
    rw = moment1.shape[0]
    nc = hid // WIDE
    nr = SUMMED * nc // 8
    any_spec, vmem = pl.BlockSpec(memory_space=pltpu.HBM), pl.BlockSpec(memory_space=pltpu.VMEM)
    dma = pltpu.SemaphoreType.DMA
    results = (((m, dw), BF16), ((g, hid), BF16), ((rw, hid), BF16), ((rw, hid), BF16), ((rw, hid), F32))
    held = pl.pallas_call(
        functools.partial(kernel, ndp, nt),
        out_shape=tuple(pltpu.VMEM(shape, dtype) for shape, dtype in results),
        in_specs=[any_spec] * 6,
        out_specs=(vmem,) * 5,
        scratch_shapes=[
            pltpu.VMEM((g, dw), BF16),
            pltpu.VMEM((nt, ndp, m, rw), BF16),
            pltpu.VMEM((nt, ndp - CORES, m, rw), BF16),
            pltpu.VMEM((rw, ndp * g), BF16),
            pltpu.VMEM((rw, (ndp - CORES) * g), BF16),
            pltpu.VMEM((nc, dw, WIDE), BF16),
            pltpu.VMEM((g, hid), BF16),
            pltpu.VMEM((g, hid), BF16),
            pltpu.VMEM((rw, hid), BF16),
            pltpu.VMEM((rw, hid), BF16),
            pltpu.VMEM((nc, ndp * g, WIDE), BF16),
            pltpu.VMEM((g, dw), BF16),
            pltpu.VMEM((nt, m, dw), BF16),
            pltpu.VMEM((nr, rw, WIDE), BF16),
            pltpu.VMEM((nr, rw, WIDE), BF16),
            dma((5,)), dma((nc,)), dma((3,)), dma((2,)), dma((6,)), dma((4,)),
            dma((2,)), dma((1,)), dma((2,)), dma((nc,)), dma((2, nc)),
            dma((nc,)), dma((nc,)), dma((1,)), dma((nr,)), dma((2,)),
        ],
        compiler_params=pltpu.CompilerParams(
            collective_id=0, has_side_effects=True, vmem_limit_bytes=VMEM_BUDGET),
    )(*(pltpu.with_memory_space_constraint(x, pltpu.HBM)
        for x in (tokens, gate_weight, up_act, cotangent, moment1, moment2)))
    return pl.pallas_call(
        write_out,
        out_shape=tuple(pltpu.HBM(shape, dtype) for shape, dtype in results),
        in_specs=[vmem] * 5,
        out_specs=(any_spec,) * 5,
        scratch_shapes=[dma((5,))],
        compiler_params=pltpu.CompilerParams(vmem_limit_bytes=2**20),
    )(*(pltpu.with_memory_space_constraint(x, pltpu.VMEM) for x in held))


def write_out(*refs):
    sems = refs[-1]
    copies = [pltpu.make_async_copy(refs[i], refs[5 + i], sems.at[i]) for i in range(5)]
    for copy in reversed(copies):
        copy.start()
    for copy in copies:
        copy.wait()


def plain(ndp, nt, tokens, gate_weight, up_act, cotangent, moment1, moment2):
    gathered = lax.all_gather(tokens, "tensor", axis=0, tiled=True)
    gate_pre = jnp.dot(gathered, gate_weight, preferred_element_type=F32)
    up_grad, gate_grad = activation_grads(gate_pre, cotangent, up_act)
    term = lax.dot_general(
        gate_grad, gate_weight, (((1,), (1,)), ((), ())), preferred_element_type=F32).astype(BF16)
    in_grad = lax.psum_scatter(term, "tensor", scatter_dimension=0, tiled=True)
    partial_value = lax.dot_general(
        gathered, gate_grad, (((0,), (0,)), ((), ())), preferred_element_type=F32).astype(BF16)
    shard = lax.psum_scatter(partial_value.astype(F32), "dp", scatter_dimension=0, tiled=True)
    first, second, update = adam(shard * (1.0 / math.sqrt(ndp * gathered.shape[0])), moment1, moment2)
    return in_grad, up_grad, first.astype(BF16), second.astype(BF16), update


def local(ndp, nt, *args):
    (m, dw), (g, hid), rw = args[0].shape, args[2].shape, args[4].shape[0]
    need = (2 * dw * hid + 2 * ndp * g * (hid + 2 * rw) + 12 * g * hid + 16 * rw * hid + 16 * g * dw)
    fits = (need <= VMEM_BUDGET and hid >= 8 * WIDE and ndp == CORES * CHIPS and nt > 1 and nt & (nt - 1) == 0
            and hid % WIDE == 0 and g % 128 == 0 and rw % 128 == 0 and m % 16 == 0
            and dw % (128 * (hid // WIDE)) == 0)
    return (fused if fits else plain)(ndp, nt, *args)


def solution(mesh):
    both = P("dp", "tensor")
    rows = P(("dp", "tensor"), None)
    return jax.shard_map(
        functools.partial(local, mesh.shape["dp"], mesh.shape["tensor"]),
        mesh=mesh,
        in_specs=(rows, P(None, "tensor"), both, both, both, both),
        out_specs=(rows, both, both, both, both),
        check_vma=False,
    )
```

time: 47.9 us -> 45.5 us (0.950)
  Pallas kernels: 47 us -> 44.7 us
    pallas_call x1, Pallas kernels: 44.8 us -> 42.5 us  [fused(): pl.pallas_call(functools.partial(kernel, ndp, nt), out_shape=tuple((pltpu...]
where the time goes in v3:
time: 45.5 us; the launch traced here: 45.3 us
  Pallas kernels  44.7 us (98%)
  between operations  0.64 us (1%)
    pallas_call x1, Pallas kernels, fused(): pl.pallas_call(functools.partial(kernel, ndp, nt), out_shape=tuple((pltpu...  42.5 us
    pallas_call x1, Pallas kernels, fused(): pl.pallas_call(write_out, out_shape=tuple((pltpu.HBM(shape, dtype) for sh...  2.24 us

profile of v3, /device:TPU:0, one launch (start us, length us, event | category | flops | bytes accessed | tf_op | source)
XLA Modules:
  0.0 45.3 jit_solution(5441490519434127910)
XLA Ops:
  0.6 42.5 %shard_map.101 = (bf16[32,2048]{1,0:T(8,128)(2,1)S(1)}, bf16[128,2048]{1,0:T(8,128)(2,1)S(1)}, bf16[256,2048]{1,0:T(8,128)(2,1)S(1)}, bf16[256,2048]{1,0:T(8,128)(2,1)S(1)}, f32[256,2048]{1,0:T(8,128)S(1)}) custom-call(bf16[32,2048]{1,0:T(8,128)(2,1)} %tok.1, bf16[2048,2048]{1,0:T(8,128)(2,1)} %w.1, bf16[128,2048]{1,0:T(8,128)(2,1)} %up.1, ...), custom_call_target="tpu_custom_call" | custom-call | tf_op jit(solution)/shard_map/pallas_call | solution.py:529
  43.1 2.2 %shard_map.102 = (bf16[32,2048]{1,0:T(8,128)(2,1)}, bf16[128,2048]{1,0:T(8,128)(2,1)}, bf16[256,2048]{1,0:T(8,128)(2,1)}, bf16[256,2048]{1,0:T(8,128)(2,1)}, f32[256,2048]{1,0:T(8,128)}) custom-call(bf16[32,2048]{1,0:T(8,128)(2,1)S(1)} %get-tuple-element.10.refs_0_, bf16[128,2048]{1,0:T(8,128)(2,1)S(1)} %get-tuple-element.11.refs_1_, ...), custom_call_target="tpu_custom_call" | custom-call | tf_op jit(solution)/shard_map/pallas_call | solution.py:558

commit v4 on v3

--- a/solution.py
+++ b/solution.py
@@ -16,6 +16,8 @@
 SUMMED = 2
 LEAD = 4
 W_DEPTH = 3
+EARLY = 3
+EARLY_LAG = 2
 VMEM_BUDGET = 48 * 2**20
 
 
@@ -61,6 +63,9 @@
     nr = part_s.shape[0]
     ng = nc - nr
     lead = min(LEAD, ng)
+    early = (nt // 2 + 1) * m
+    A, B, B_EARLY, B_LATE = (0, m), (m, g), (m, early), (early, g)
+    ns = min(EARLY, ng - EARLY_LAG)
     scale = 1.0 / math.sqrt(ndp * g)
 
     half = z // 2
@@ -110,9 +115,12 @@
             pltpu.make_async_copy(up.at[m:g], upv.at[m:g], cu_sem.at[2]).wait()
 
     def tok_copy(k):
-        return rdma(tg.at[0:m], tg.at[k * m:(k + 1) * m], tok_sem.at[0], tok_sem.at[1], d, flip(t, k))
+        return rdma(tg.at[0:m], tg.at[k * m:(k + 1) * m], tok_sem.at[0],
+                    tok_sem.at[1 if k * m < early else 2], d, flip(t, k))
 
     tok_all = rdma(tg.at[m:g], tg.at[m:g], tok_sem.at[0], tok_sem.at[1], mate, t)
+    tok_early = rdma(tg.at[m:early], tg.at[m:early], tok_sem.at[0], tok_sem.at[1], mate, t)
+    tok_late = rdma(tg.at[early:g], tg.at[early:g], tok_sem.at[0], tok_sem.at[2], mate, t)
 
     def features(chip, cr):
         return tg.at[0:m, rows_of(chip * CORES + cr, rw)]
@@ -152,30 +160,32 @@
     def replica(c, chip, cr):
         return gall.at[c, rows_of(chip * CORES + cr, g)]
 
-    def block(c, part, chip, cr):
-        start = pl.multiple_of((chip * CORES + cr) * g, g) + (m if part else 0)
-        return gall.at[c, pl.ds(pl.multiple_of(start, m), g - m if part else m)]
-
-    def to_near(c, part):
-        b = block(c, part, z, core)
+    def span_of(index, rows):
+        return pl.ds(pl.multiple_of(index * g + rows[0], m), rows[1] - rows[0])
+
+    def block(c, rows, chip):
+        return gall.at[c, span_of(chip * CORES + core, rows)]
+
+    def to_near(c, rows):
+        b = block(c, rows, z)
         return rdma(b, b, zs.at[0], zr_near.at[c], near * CORES + core, t)
 
-    def to_across(c, part):
-        b = block(c, part, z, core)
-        return rdma(b, b, zs.at[1], zr_rest.at[part, c], across * CORES + core, t)
+    def to_across(c, rows):
+        b = block(c, rows, z)
+        return rdma(b, b, zs.at[1], zr_rest.at[0 if rows == A else 1, c], across * CORES + core, t)
 
     def near_in(c):
         b = replica(c, near, core)
         rdma(b, b, zs.at[0], zr_near.at[c], near * CORES + core, t).wait_recv()
 
-    def rest_in(c, part):
-        b = gall.at[c, 0:2 * (g - m if part else m)]
-        rdma(b, b, zs.at[0], zr_rest.at[part, c], near * CORES + core, t).wait_recv()
-
-    def forward(c, part):
+    def rest_in(c, rows):
+        b = gall.at[c, 0:2 * (rows[1] - rows[0])]
+        rdma(b, b, zs.at[0], zr_rest.at[0 if rows == A else 1, c], near * CORES + core, t).wait_recv()
+
+    def forward(c, rows):
         for chip in (across, far):
-            b = block(c, part, chip, core)
-            rdma(b, b, fs.at[0], zr_rest.at[part, c], near * CORES + core, t).start()
+            b = block(c, rows, chip)
+            rdma(b, b, fs.at[0], zr_rest.at[0 if rows == A else 1, c], near * CORES + core, t).start()
 
     def mate_copy(c, chip):
         b = replica(c, chip, core)
@@ -194,25 +204,29 @@
     def part_copy(j):
         return rdma(part_s.at[j], part_r.at[j], rs.at[0], rr.at[j], served, t)
 
-    def grads(c, part):
-        here = slice(m, g) if part else slice(0, m)
+    def grads(c, rows):
+        here = slice(*rows)
         cols = rows_of(c, hc)
         gate_pre = jnp.dot(tg[here], wv[c], preferred_element_type=F32)
         ug, gg = activation_grads(gate_pre, cotv[here, cols], upv[here, cols])
-        start = pl.multiple_of(d * g, g) + (m if part else 0)
-        gall[c, pl.ds(pl.multiple_of(start, m), g - m if part else m), :] = gg
-        for k in range(1, nt) if part else (0,):
-            low = (k - 1) * m if part else 0
+        gall[c, span_of(d, rows), :] = gg
+        for k in range(rows[0] // m, rows[1] // m):
+            low = k * m - rows[0]
             up_grad[rows_of(flip(t, k), m), cols] = ug[low:low + m]
 
-    def send_own(c, part):
-        to_across(c, part).start()
-
+    def send_near(c, rows):
         @pl.when(jnp.logical_or(outer == 1, c < ng))
         def _():
-            to_near(c, part).start()
-        if part:
-            mate_copy(c, z).start()
+            to_near(c, rows).start()
+
+    def send_first(c):
+        to_across(c, A).start()
+        send_near(c, A)
+
+    def send_rest(c, near_rows=B):
+        send_near(c, near_rows)
+        to_across(c, B).start()
+        mate_copy(c, z).start()
 
     span = dw // nc
 
@@ -300,15 +314,18 @@
             @pl.when(c + depth < nc)
             def _():
                 w_load(c + depth).start()
-            grads(c, 0)
+
+            @pl.when(c == nc // 2)
+            def _():
+                for k in range(1, nt):
+                    for copy in cu_loads(k):
+                        copy.start()
+            grads(c, A)
 
             @pl.when(jnp.logical_and(c > 0, c <= ng))
             def _():
-                send_own(c - 1, 0)
-
-    for k in range(1, nt):
-        for copy in cu_loads(k):
-            copy.start()
+                send_first(c - 1)
+
     load_x.start()
     inner_only(load_xp.start)
     load_m1.start()
@@ -323,36 +340,73 @@
 
     @pl.loop(ng, nc)
     def _(c):
-        send_own(c, 0)
+        send_first(c)
 
     @phase
     def inner_forwards():
         @inner_only
         def _():
-            @pl.loop(0, ng)
+            @pl.loop(0, EARLY_LAG)
             def _(c):
-                rest_in(c, 0)
-                forward(c, 0)
+                rest_in(c, A)
+                forward(c, A)
+            cu_wait(False)
+            tok_early.wait_recv()
+
+            @pl.loop(0, ns)
+            def _(c):
+                grads(c, B_EARLY)
+                rest_in(EARLY_LAG + c, A)
+                forward(EARLY_LAG + c, A)
+                to_near(c, B_EARLY).start()
+
+            @pl.loop(EARLY_LAG + ns, ng)
+            def _(c):
+                rest_in(c, A)
+                forward(c, A)
+
+        @outer_only
+        def _():
+            cu_wait(False)
+            tok_early.wait_recv()
 
     @phase
     def tok_wait():
-        cu_wait(False)
-        tok_all.wait_recv()
+        tok_late.wait_recv()
 
     @phase
     def other_grads():
-        @pl.loop(0, nc)
+        @inner_only
+        def _():
+            @pl.loop(0, ns)
+            def _(c):
+                grads(c, B_LATE)
+
+                @pl.when(c > 0)
+                def _():
+                    send_rest(c - 1, B_LATE)
+            grads(ns, B)
+            send_rest(ns - 1, B_LATE)
+
+        @outer_only
+        def _():
+            @pl.loop(0, ns + 1)
+            def _(c):
+                grads(c, B)
+
+                @pl.when(c > 0)
+                def _():
+                    send_rest(c - 1)
+
+        @pl.loop(ns + 1, nc)
         def _(c):
-            grads(c, 1)
-
-            @pl.when(c > 0)
-            def _():
-                send_own(c - 1, 1)
+            grads(c, B)
+            send_rest(c - 1)
 
     @phase
     def x_exchange():
         term_part(0)
-        send_own(nc - 1, 1)
+        send_rest(nc - 1)
         load_x.wait()
 
         @inner_only
@@ -391,12 +445,12 @@
 
             @outer_only
             def _():
-                rest_in(c, 0)
-            rest_in(c, 1)
+                rest_in(c, A)
+            rest_in(c, B)
 
             @inner_only
             def _():
-                forward(c, 1)
+                forward(c, B)
             mate_copy(c, across).start()
             mate_copy(c, far).start()
 
@@ -448,8 +502,8 @@
         for j in range(nr):
             @phase
             def last_in():
-                rest_in(ng + j, 0)
-                rest_in(ng + j, 1)
+                rest_in(ng + j, A)
+                rest_in(ng + j, B)
                 mate_copy(ng + j, across).start()
                 mate_copy(ng + j, far).start()
 
@@ -547,7 +601,7 @@
             pltpu.VMEM((nt, m, dw), BF16),
             pltpu.VMEM((nr, rw, WIDE), BF16),
             pltpu.VMEM((nr, rw, WIDE), BF16),
-            dma((5,)), dma((nc,)), dma((3,)), dma((2,)), dma((6,)), dma((4,)),
+            dma((5,)), dma((nc,)), dma((3,)), dma((3,)), dma((6,)), dma((4,)),
             dma((2,)), dma((1,)), dma((2,)), dma((nc,)), dma((2, nc)),
             dma((nc,)), dma((nc,)), dma((1,)), dma((nr,)), dma((2,)),
         ],

time: 45.5 us -> 45 us (0.989)
  Pallas kernels: 44.7 us -> 44.2 us
    pallas_call x1, Pallas kernels: 42.5 us -> 41.9 us  [fused(): pl.pallas_call(functools.partial(kernel, ndp, nt), out_shape=tuple((pltpu...]
where the time goes in v4:
time: 45 us; the launch traced here: 44.8 us
  Pallas kernels  44.2 us (98%)
  between operations  0.64 us (1%)
    pallas_call x1, Pallas kernels, fused(): pl.pallas_call(functools.partial(kernel, ndp, nt), out_shape=tuple((pltpu...  41.9 us
    pallas_call x1, Pallas kernels, fused(): pl.pallas_call(write_out, out_shape=tuple((pltpu.HBM(shape, dtype) for sh...  2.24 us

profile of v4, /device:TPU:0, one launch (start us, length us, event | category | flops | bytes accessed | tf_op | source)
XLA Modules:
  0.0 44.8 jit_solution(17813893570755904869)
XLA Ops:
  0.6 41.9 %shard_map.101 = (bf16[32,2048]{1,0:T(8,128)(2,1)S(1)}, bf16[128,2048]{1,0:T(8,128)(2,1)S(1)}, bf16[256,2048]{1,0:T(8,128)(2,1)S(1)}, bf16[256,2048]{1,0:T(8,128)(2,1)S(1)}, f32[256,2048]{1,0:T(8,128)S(1)}) custom-call(bf16[32,2048]{1,0:T(8,128)(2,1)} %tok.1, bf16[2048,2048]{1,0:T(8,128)(2,1)} %w.1, bf16[128,2048]{1,0:T(8,128)(2,1)} %up.1, ...), custom_call_target="tpu_custom_call" | custom-call | tf_op jit(solution)/shard_map/pallas_call | solution.py:583
  42.6 2.2 %shard_map.102 = (bf16[32,2048]{1,0:T(8,128)(2,1)}, bf16[128,2048]{1,0:T(8,128)(2,1)}, bf16[256,2048]{1,0:T(8,128)(2,1)}, bf16[256,2048]{1,0:T(8,128)(2,1)}, f32[256,2048]{1,0:T(8,128)}) custom-call(bf16[32,2048]{1,0:T(8,128)(2,1)S(1)} %get-tuple-element.10.refs_0_, bf16[128,2048]{1,0:T(8,128)(2,1)S(1)} %get-tuple-element.11.refs_1_, ...), custom_call_target="tpu_custom_call" | custom-call | tf_op jit(solution)/shard_map/pallas_call | solution.py:612

commit v5 on v4

--- a/solution.py
+++ b/solution.py
@@ -16,6 +16,7 @@
 SUMMED = 2
 LEAD = 4
 W_DEPTH = 3
+ALONE = 3
 EARLY = 3
 EARLY_LAG = 2
 VMEM_BUDGET = 48 * 2**20
@@ -52,7 +53,7 @@
 def kernel(ndp, nt, tok, w, up, cot, m1, m2, in_grad, up_grad, nm1, nm2, upd,
            tg, xg, xp, xt, xtp, wv, upv, cotv, m1v, m2v, gall, term, termr, part_s, part_r,
            loc_sem, w_sem, cu_sem, tok_sem, x_sem, x2_sem, zs, fs, ms, zr_near, zr_rest,
-           mr_near, mr_rest, rs, rr, term_sem):
+           mr_near, mr_rest, rs, rr, term_sem, go):
     d, t = lax.axis_index("dp"), lax.axis_index("tensor")
     z, core = d // CORES, lax.rem(d, CORES)
     mate = d + 1 - 2 * core
@@ -268,61 +269,154 @@
     depth = min(W_DEPTH, nc)
 
     load_tok.start()
+    for copy in cu_loads(0):
+        copy.start()
+    w_load(0).start()
     barrier = pltpu.get_barrier_semaphore()
-
-    def greet(dp, tn):
-        pl.semaphore_signal(barrier, inc=1, device_id=(dp, tn), device_id_type=MESH)
-
+    even = lax.rem(z, 2) == 0
+    NEAR, ACROSS, PEERS, MATE = range(4)
+
+    def tell(sem, chip):
+        for cr in range(CORES):
+            pl.semaphore_signal(sem, inc=1, device_id=(chip * CORES + cr, t), device_id_type=MESH)
+
+    @pl.when(even)
+    def _():
+        tell(barrier, near)
+
+    @pl.when(half == 0)
+    def _():
+        tell(barrier, across)
+
+        @inner_only
+        def _():
+            tell(barrier, far)
+
+    @pl.when(core == 0)
+    def _():
+        pl.semaphore_signal(barrier, inc=1, device_id=(mate, t), device_id_type=MESH)
     for k in range(1, nt):
-        greet(d, flip(t, k))
-    greet(mate, t)
-    for cr in range(CORES):
-        greet(near * CORES + cr, t)
-
-    @inner_only
-    def _():
-        for chip in (across, far):
-            for cr in range(CORES):
-                greet(chip * CORES + cr, t)
+        @pl.when(flip(t, k) > t)
+        def _():
+            pl.semaphore_signal(barrier, inc=1, device_id=(d, flip(t, k)), device_id_type=MESH)
 
     @phase
     def tok_load():
         load_tok.wait()
 
-    for copy in cu_loads(0):
-        copy.start()
-    for c in range(depth):
+    for c in range(1, depth):
         w_load(c).start()
 
     @phase
     def meet():
-        pl.semaphore_wait(barrier, nt - 1 + 1 + 2 * CORES)
-
+        earlier = CORES * (z - half * lax.rem(z, 2)) + t + core
+
+        @pl.when(earlier > 0)
+        def _():
+            pl.semaphore_wait(barrier, earlier)
+
+    @pl.when(jnp.logical_not(even))
+    def _():
+        tell(go.at[NEAR], near)
+
+    @pl.when(half == 1)
+    def _():
+        @inner_only
+        def _():
+            tell(go.at[ACROSS], across)
+            tell(go.at[ACROSS], far)
+
+    @pl.when(core == 1)
+    def _():
+        pl.semaphore_signal(go.at[MATE], inc=1, device_id=(mate, t), device_id_type=MESH)
     for k in range(1, nt):
-        tok_copy(k).start()
+        @pl.when(flip(t, k) < t)
+        def _():
+            pl.semaphore_signal(go.at[PEERS], inc=1, device_id=(d, flip(t, k)), device_id_type=MESH)
+            tok_copy(k).start()
+
+    def send_down(c):
+        @pl.when(half == 1)
+        def _():
+            to_across(c, A).start()
+
+        @pl.when(jnp.logical_not(even))
+        def _():
+            send_near(c, A)
+
+    def send_up(c):
+        @pl.when(half == 0)
+        def _():
+            to_across(c, A).start()
+
+        @pl.when(even)
+        def _():
+            send_near(c, A)
+
+    def own_chunk(c):
+        w_load(c).wait()
+
+        @pl.when(c + depth < nc)
+        def _():
+            w_load(c + depth).start()
+
+        @pl.when(c == nc // 2)
+        def _():
+            for k in range(1, nt):
+                for copy in cu_loads(k):
+                    copy.start()
+        grads(c, A)
 
     @phase
     def own_loads():
         cu_wait(True)
 
+    alone = min(ALONE, ng)
+
+    @phase
+    def own_first():
+        @pl.loop(0, alone)
+        def _(c):
+            own_chunk(c)
+
+            @pl.when(c > 0)
+            def _():
+                send_down(c - 1)
+
+    @phase
+    def go_wait():
+        @pl.when(t < nt - 1)
+        def _():
+            pl.semaphore_wait(go.at[PEERS], nt - 1 - t)
+        for k in range(1, nt):
+            @pl.when(flip(t, k) > t)
+            def _():
+                tok_copy(k).start()
+        send_down(alone - 1)
+
+        @pl.when(even)
+        def _():
+            pl.semaphore_wait(go.at[NEAR], CORES)
+
+        @pl.when(half == 0)
+        def _():
+            pl.semaphore_wait(go.at[ACROSS], CORES)
+
+        @pl.when(core == 0)
+        def _():
+            pl.semaphore_wait(go.at[MATE], 1)
+
+        @pl.loop(0, alone)
+        def _(c):
+            send_up(c)
+
     @phase
     def own_grads():
-        @pl.loop(0, nc)
+        @pl.loop(alone, nc)
         def _(c):
-            w_load(c).wait()
-
-            @pl.when(c + depth < nc)
-            def _():
-                w_load(c + depth).start()
-
-            @pl.when(c == nc // 2)
-            def _():
-                for k in range(1, nt):
-                    for copy in cu_loads(k):
-                        copy.start()
-            grads(c, A)
-
-            @pl.when(jnp.logical_and(c > 0, c <= ng))
+            own_chunk(c)
+
+            @pl.when(jnp.logical_and(c > alone, c <= ng))
             def _():
                 send_first(c - 1)
 
@@ -350,8 +444,11 @@
             def _(c):
                 rest_in(c, A)
                 forward(c, A)
-            cu_wait(False)
-            tok_early.wait_recv()
+
+            @phase
+            def early_wait():
+                cu_wait(False)
+                tok_early.wait_recv()
 
             @pl.loop(0, ns)
             def _(c):
@@ -603,7 +700,7 @@
             pltpu.VMEM((nr, rw, WIDE), BF16),
             dma((5,)), dma((nc,)), dma((3,)), dma((3,)), dma((6,)), dma((4,)),
             dma((2,)), dma((1,)), dma((2,)), dma((nc,)), dma((2, nc)),
-            dma((nc,)), dma((nc,)), dma((1,)), dma((nr,)), dma((2,)),
+            dma((nc,)), dma((nc,)), dma((1,)), dma((nr,)), dma((2,)), pltpu.SemaphoreType.REGULAR((4,)),
         ],
         compiler_params=pltpu.CompilerParams(
             collective_id=0, has_side_effects=True, vmem_limit_bytes=VMEM_BUDGET),

time: 45 us -> 44.8 us (level)
  no operation moved by 1% of the time
where the time goes in v5:
time: 44.8 us; the launch traced here: 44.4 us
  Pallas kernels  43.8 us (98%)
  between operations  0.64 us (1%)
    pallas_call x1, Pallas kernels, fused(): pl.pallas_call(functools.partial(kernel, ndp, nt), out_shape=tuple((pltpu...  41.5 us
    pallas_call x1, Pallas kernels, fused(): pl.pallas_call(write_out, out_shape=tuple((pltpu.HBM(shape, dtype) for sh...  2.24 us

profile of v5, /device:TPU:0, one launch (start us, length us, event | category | flops | bytes accessed | tf_op | source)
XLA Modules:
  0.0 44.4 jit_solution(9747205268887557782)
XLA Ops:
  0.6 41.5 %shard_map.101 = (bf16[32,2048]{1,0:T(8,128)(2,1)S(1)}, bf16[128,2048]{1,0:T(8,128)(2,1)S(1)}, bf16[256,2048]{1,0:T(8,128)(2,1)S(1)}, bf16[256,2048]{1,0:T(8,128)(2,1)S(1)}, f32[256,2048]{1,0:T(8,128)S(1)}) custom-call(bf16[32,2048]{1,0:T(8,128)(2,1)} %tok.1, bf16[2048,2048]{1,0:T(8,128)(2,1)} %w.1, bf16[128,2048]{1,0:T(8,128)(2,1)} %up.1, ...), custom_call_target="tpu_custom_call" | custom-call | tf_op jit(solution)/shard_map/pallas_call | solution.py:680
  42.2 2.2 %shard_map.102 = (bf16[32,2048]{1,0:T(8,128)(2,1)}, bf16[128,2048]{1,0:T(8,128)(2,1)}, bf16[256,2048]{1,0:T(8,128)(2,1)}, bf16[256,2048]{1,0:T(8,128)(2,1)}, f32[256,2048]{1,0:T(8,128)}) custom-call(bf16[32,2048]{1,0:T(8,128)(2,1)S(1)} %get-tuple-element.10.refs_0_, bf16[128,2048]{1,0:T(8,128)(2,1)S(1)} %get-tuple-element.11.refs_1_, ...), custom_call_target="tpu_custom_call" | custom-call | tf_op jit(solution)/shard_map/pallas_call | solution.py:709

commit v6 on v5

--- a/solution.py
+++ b/solution.py
@@ -16,7 +16,7 @@
 SUMMED = 2
 LEAD = 4
 W_DEPTH = 3
-ALONE = 3
+ALONE = 2
 EARLY = 3
 EARLY_LAG = 2
 VMEM_BUDGET = 48 * 2**20
@@ -53,7 +53,7 @@
 def kernel(ndp, nt, tok, w, up, cot, m1, m2, in_grad, up_grad, nm1, nm2, upd,
            tg, xg, xp, xt, xtp, wv, upv, cotv, m1v, m2v, gall, term, termr, part_s, part_r,
            loc_sem, w_sem, cu_sem, tok_sem, x_sem, x2_sem, zs, fs, ms, zr_near, zr_rest,
-           mr_near, mr_rest, rs, rr, term_sem, go):
+           mr, rs, rr, term_sem, go):
     d, t = lax.axis_index("dp"), lax.axis_index("tensor")
     z, core = d // CORES, lax.rem(d, CORES)
     mate = d + 1 - 2 * core
@@ -100,7 +100,7 @@
     load_m2 = pltpu.make_async_copy(m2, m2v, loc_sem.at[3])
 
     def w_load(c):
-        return pltpu.make_async_copy(w.at[:, rows_of(c, hc)], wv.at[c], w_sem.at[c])
+        return pltpu.make_async_copy(w.at[:, rows_of(c, hc)], wv.at[c], w_sem.at[lax.rem(c, W_DEPTH)])
 
     def cu_loads(k):
         src = rows_of(flip(t, k), m)
@@ -190,17 +190,15 @@
 
     def mate_copy(c, chip):
         b = replica(c, chip, core)
-        if chip is near:
-            return rdma(b, b, ms.at[1], mr_near.at[c], mate, t)
-        return rdma(b, b, ms.at[0 if chip is z else 1], mr_rest.at[c], mate, t)
-
-    def mate_near_in(c):
-        b = gall.at[c, 0:g]
-        rdma(b, b, ms.at[0], mr_near.at[c], mate, t).wait_recv()
-
-    def mate_rest_in(c, replicas):
-        b = gall.at[c, 0:replicas * g]
-        rdma(b, b, ms.at[0], mr_rest.at[c], mate, t).wait_recv()
+        return rdma(b, b, ms.at[0 if chip is z else 1], mr.at[c], mate, t)
+
+    def mate_last(j):
+        b = replica(ng + j, near, core)
+        return rdma(b, b, ms.at[1], mr.at[nc + j], mate, t)
+
+    def mate_in(c, replicas):
+        b = gall.at[0, 0:replicas * g]
+        rdma(b, b, ms.at[0], mr.at[c], mate, t).wait_recv()
 
     def part_copy(j):
         return rdma(part_s.at[j], part_r.at[j], rs.at[0], rr.at[j], served, t)
@@ -248,25 +246,26 @@
         upd[:, cols] = change
 
     def update(c, reduced=False):
-        mate_near_in(c)
-        if not reduced:
-            mate_rest_in(c, 3)
+        if reduced:
+            mate_in(c + nr, 1)
+        else:
+            mate_in(c, 4)
         step(c, jnp.dot(xt[...], gall[c], preferred_element_type=F32))
 
     def reduce(c, j):
-        mate_rest_in(c, 3)
+        mate_in(c, 3)
         rows = pl.ds(pl.multiple_of(first_rep * g, g), others * g)
         part_s[j] = jnp.dot(xtp[...], gall[c, rows, :], preferred_element_type=F32).astype(BF16)
         part_copy(j).start()
 
     def finish(c, j):
-        mate_rest_in(c, 1)
+        mate_in(c, 1)
         own = rows_of(z, CORES * g)
         grad = jnp.dot(xt[:, own], gall[c, own, :], preferred_element_type=F32)
         part_copy(j).wait_recv()
         step(c, grad + part_r[j].astype(F32))
 
-    depth = min(W_DEPTH, nc)
+    depth = W_DEPTH
 
     load_tok.start()
     for copy in cu_loads(0):
@@ -274,7 +273,7 @@
     w_load(0).start()
     barrier = pltpu.get_barrier_semaphore()
     even = lax.rem(z, 2) == 0
-    NEAR, ACROSS, PEERS, MATE = range(4)
+    NEAR, ACROSS, MATE = range(3)
 
     def tell(sem, chip):
         for cr in range(CORES):
@@ -301,13 +300,6 @@
             pl.semaphore_signal(barrier, inc=1, device_id=(d, flip(t, k)), device_id_type=MESH)
 
     @phase
-    def tok_load():
-        load_tok.wait()
-
-    for c in range(1, depth):
-        w_load(c).start()
-
-    @phase
     def meet():
         earlier = CORES * (z - half * lax.rem(z, 2)) + t + core
 
@@ -332,8 +324,17 @@
     for k in range(1, nt):
         @pl.when(flip(t, k) < t)
         def _():
-            pl.semaphore_signal(go.at[PEERS], inc=1, device_id=(d, flip(t, k)), device_id_type=MESH)
-            tok_copy(k).start()
+            pl.semaphore_signal(go.at[MATE + k], inc=1, device_id=(d, flip(t, k)), device_id_type=MESH)
+
+    @phase
+    def tok_load():
+        load_tok.wait()
+
+    for c in range(1, depth):
+        w_load(c).start()
+
+    for k in range(1, nt):
+        pl.when(flip(t, k) < t)(tok_copy(k).start)
 
     def send_down(c):
         @pl.when(half == 1)
@@ -385,12 +386,10 @@
 
     @phase
     def go_wait():
-        @pl.when(t < nt - 1)
-        def _():
-            pl.semaphore_wait(go.at[PEERS], nt - 1 - t)
         for k in range(1, nt):
             @pl.when(flip(t, k) > t)
             def _():
+                pl.semaphore_wait(go.at[MATE + k], 1)
                 tok_copy(k).start()
         send_down(alone - 1)
 
@@ -615,7 +614,7 @@
             @phase
             def near_last():
                 near_in(ng + j)
-                mate_copy(ng + j, near).start()
+                mate_last(j).start()
 
         @pl.loop(ng - lead + nr, ng)
         def _(c):
@@ -698,9 +697,9 @@
             pltpu.VMEM((nt, m, dw), BF16),
             pltpu.VMEM((nr, rw, WIDE), BF16),
             pltpu.VMEM((nr, rw, WIDE), BF16),
-            dma((5,)), dma((nc,)), dma((3,)), dma((3,)), dma((6,)), dma((4,)),
+            dma((5,)), dma((W_DEPTH,)), dma((3,)), dma((3,)), dma((6,)), dma((4,)),
             dma((2,)), dma((1,)), dma((2,)), dma((nc,)), dma((2, nc)),
-            dma((nc,)), dma((nc,)), dma((1,)), dma((nr,)), dma((2,)), pltpu.SemaphoreType.REGULAR((4,)),
+            dma((nc + nr,)), dma((1,)), dma((nr,)), dma((2,)), pltpu.SemaphoreType.REGULAR((2 + nt,)),
         ],
         compiler_params=pltpu.CompilerParams(
             collective_id=0, has_side_effects=True, vmem_limit_bytes=VMEM_BUDGET),

time: 44.8 us -> 44.5 us (level)
  no operation moved by 1% of the time
where the time goes in v6:
time: 44.5 us; the launch traced here: 44.3 us
  Pallas kernels  43.7 us (98%)
  between operations  0.64 us (1%)
    pallas_call x1, Pallas kernels, fused(): pl.pallas_call(functools.partial(kernel, ndp, nt), out_shape=tuple((pltpu...  41.5 us
    pallas_call x1, Pallas kernels, fused(): pl.pallas_call(write_out, out_shape=tuple((pltpu.HBM(shape, dtype) for sh...  2.24 us

profile of v6, /device:TPU:0, one launch (start us, length us, event | category | flops | bytes accessed | tf_op | source)
XLA Modules:
  0.0 44.3 jit_solution(6253525145058899370)
XLA Ops:
  0.6 41.5 %shard_map.101 = (bf16[32,2048]{1,0:T(8,128)(2,1)S(1)}, bf16[128,2048]{1,0:T(8,128)(2,1)S(1)}, bf16[256,2048]{1,0:T(8,128)(2,1)S(1)}, bf16[256,2048]{1,0:T(8,128)(2,1)S(1)}, f32[256,2048]{1,0:T(8,128)S(1)}) custom-call(bf16[32,2048]{1,0:T(8,128)(2,1)} %tok.1, bf16[2048,2048]{1,0:T(8,128)(2,1)} %w.1, bf16[128,2048]{1,0:T(8,128)(2,1)} %up.1, ...), custom_call_target="tpu_custom_call" | custom-call | tf_op jit(solution)/shard_map/pallas_call | solution.py:679
  42.1 2.2 %shard_map.102 = (bf16[32,2048]{1,0:T(8,128)(2,1)}, bf16[128,2048]{1,0:T(8,128)(2,1)}, bf16[256,2048]{1,0:T(8,128)(2,1)}, bf16[256,2048]{1,0:T(8,128)(2,1)}, f32[256,2048]{1,0:T(8,128)}) custom-call(bf16[32,2048]{1,0:T(8,128)(2,1)S(1)} %get-tuple-element.10.refs_0_, bf16[128,2048]{1,0:T(8,128)(2,1)S(1)} %get-tuple-element.11.refs_1_, ...), custom_call_target="tpu_custom_call" | custom-call | tf_op jit(solution)/shard_map/pallas_call | solution.py:708

commit v7 on v6

--- a/solution.py
+++ b/solution.py
@@ -17,7 +17,7 @@
 LEAD = 4
 W_DEPTH = 3
 ALONE = 2
-EARLY = 3
+EARLY = 4
 EARLY_LAG = 2
 VMEM_BUDGET = 48 * 2**20
 
@@ -200,8 +200,10 @@
         b = gall.at[0, 0:replicas * g]
         rdma(b, b, ms.at[0], mr.at[c], mate, t).wait_recv()
 
-    def part_copy(j):
-        return rdma(part_s.at[j], part_r.at[j], rs.at[0], rr.at[j], served, t)
+    halves = [slice(0, rw // 2), slice(rw // 2, rw)]
+
+    def part_copy(j, h):
+        return rdma(part_s.at[j, halves[h]], part_r.at[j, halves[h]], rs.at[0], rr.at[j, h], served, t)
 
     def grads(c, rows):
         here = slice(*rows)
@@ -238,12 +240,12 @@
                 gall[c, own, :], wv[c, rows, :], (((1,), (1,)), ((), ())), preferred_element_type=F32)
         term[:, rows] = total.astype(BF16)
 
-    def step(c, grad):
+    def step(c, grad, rows=slice(None)):
         cols = rows_of(c, hc)
-        first, second, change = adam(grad * scale, m1v[:, cols], m2v[:, cols])
-        nm1[:, cols] = first.astype(BF16)
-        nm2[:, cols] = second.astype(BF16)
-        upd[:, cols] = change
+        first, second, change = adam(grad * scale, m1v[rows, cols], m2v[rows, cols])
+        nm1[rows, cols] = first.astype(BF16)
+        nm2[rows, cols] = second.astype(BF16)
+        upd[rows, cols] = change
 
     def update(c, reduced=False):
         if reduced:
@@ -255,15 +257,18 @@
     def reduce(c, j):
         mate_in(c, 3)
         rows = pl.ds(pl.multiple_of(first_rep * g, g), others * g)
-        part_s[j] = jnp.dot(xtp[...], gall[c, rows, :], preferred_element_type=F32).astype(BF16)
-        part_copy(j).start()
+        for h, part in enumerate(halves):
+            part_s[j, part, :] = jnp.dot(
+                xtp[part, :], gall[c, rows, :], preferred_element_type=F32).astype(BF16)
+            part_copy(j, h).start()
 
     def finish(c, j):
         mate_in(c, 1)
         own = rows_of(z, CORES * g)
         grad = jnp.dot(xt[:, own], gall[c, own, :], preferred_element_type=F32)
-        part_copy(j).wait_recv()
-        step(c, grad + part_r[j].astype(F32))
+        for h, part in enumerate(halves):
+            part_copy(j, h).wait_recv()
+            step(c, grad[part] + part_r[j, part, :].astype(F32), part)
 
     depth = W_DEPTH
 
@@ -699,7 +704,7 @@
             pltpu.VMEM((nr, rw, WIDE), BF16),
             dma((5,)), dma((W_DEPTH,)), dma((3,)), dma((3,)), dma((6,)), dma((4,)),
             dma((2,)), dma((1,)), dma((2,)), dma((nc,)), dma((2, nc)),
-            dma((nc + nr,)), dma((1,)), dma((nr,)), dma((2,)), pltpu.SemaphoreType.REGULAR((2 + nt,)),
+            dma((nc + nr,)), dma((1,)), dma((nr, 2)), dma((2,)), pltpu.SemaphoreType.REGULAR((2 + nt,)),
         ],
         compiler_params=pltpu.CompilerParams(
             collective_id=0, has_side_effects=True, vmem_limit_bytes=VMEM_BUDGET),

time: 44.5 us -> 44.3 us (level)
  no operation moved by 1% of the time
where the time goes in v7:
time: 44.3 us; the launch traced here: 44.1 us
  Pallas kernels  43.5 us (98%)
  between operations  0.64 us (1%)
    pallas_call x1, Pallas kernels, fused(): pl.pallas_call(functools.partial(kernel, ndp, nt), out_shape=tuple((pltpu...  41.2 us
    pallas_call x1, Pallas kernels, fused(): pl.pallas_call(write_out, out_shape=tuple((pltpu.HBM(shape, dtype) for sh...  2.24 us

profile of v7, /device:TPU:0, one launch (start us, length us, event | category | flops | bytes accessed | tf_op | source)
XLA Modules:
  0.0 44.1 jit_solution(9256202368942971543)
XLA Ops:
  0.6 41.2 %shard_map.101 = (bf16[32,2048]{1,0:T(8,128)(2,1)S(1)}, bf16[128,2048]{1,0:T(8,128)(2,1)S(1)}, bf16[256,2048]{1,0:T(8,128)(2,1)S(1)}, bf16[256,2048]{1,0:T(8,128)(2,1)S(1)}, f32[256,2048]{1,0:T(8,128)S(1)}) custom-call(bf16[32,2048]{1,0:T(8,128)(2,1)} %tok.1, bf16[2048,2048]{1,0:T(8,128)(2,1)} %w.1, bf16[128,2048]{1,0:T(8,128)(2,1)} %up.1, ...), custom_call_target="tpu_custom_call" | custom-call | tf_op jit(solution)/shard_map/pallas_call | solution.py:684
  41.9 2.2 %shard_map.102 = (bf16[32,2048]{1,0:T(8,128)(2,1)}, bf16[128,2048]{1,0:T(8,128)(2,1)}, bf16[256,2048]{1,0:T(8,128)(2,1)}, bf16[256,2048]{1,0:T(8,128)(2,1)}, f32[256,2048]{1,0:T(8,128)}) custom-call(bf16[32,2048]{1,0:T(8,128)(2,1)S(1)} %get-tuple-element.10.refs_0_, bf16[128,2048]{1,0:T(8,128)(2,1)S(1)} %get-tuple-element.11.refs_1_, ...), custom_call_target="tpu_custom_call" | custom-call | tf_op jit(solution)/shard_map/pallas_call | solution.py:713
